TPU v7x, 512 devices: a 8x2x16 block of a 8x8x16 slice. The times are simulated.
512 devices in a mesh: grp: 2 (over y), gz: 16 (over z), gy: 8 (over x), sa: 2 (over core).
Axes of the slice: x: 8, y: 2, z: 16, core: 2. Of those that a mesh axis runs over, the one named last changes fastest.
The devices are a block of a 8x8x16 slice.
Arguments:
- field: float32 [8, 128, 64, 128], P('sa', ('grp', 'gz'), 'gy'), parts along dimension 1, may hold values from 0 to 2
- diffusion: float32 [8], P('sa'), may hold values from 0.02 to 0.16
- secrete: float32 [8, 1048576], P('sa', ('grp', 'gz', 'gy')), parts along dimension 1, may hold values from 0 to 1
- uptake: float32 [8, 1048576], P('sa', ('grp', 'gz', 'gy')), parts along dimension 1, may hold values from 0.05 to 1
- cell_voxel: int32 [1048576], P(('grp', 'gz', 'gy')), parts along dimension 0, may hold values from 0 to 4095
- block_dest: int32 [8192, 1], P(('grp', 'gz', 'gy')), parts along dimension 0, may hold values from 0 to 15; in each aligned block of 32 rows (0 to 31, 32 to 63, ...) at most 6 rows name the same one
Outputs:
- new_field: float32 [8, 128, 64, 128], P('sa', ('grp', 'gz'), 'gy'), parts along dimension 1
- cell_conc: float32 [8, 1048576], P('sa', ('grp', 'gz', 'gy')), parts along dimension 1
There are 2 independent parts, one for each index of `grp`. A program takes and returns all parts, laid end to end along the dimension named above; an argument that names none is the same for every part. Nothing has to cross between parts.
Inputs may be any that keep to these rules, and one draw needn't show every extreme that they name: `block_dest`: among the 32 blocks of one device at most 6 name the same destination, and in every draw some device has exactly 6 blocks naming one destination.
All inputs are finite; a program needn't handle non-finite values.
Results may differ from a plain program's by a relative error of at most 0.00007.
Values sent between devices are 32-bit elements; how exact they have to be, the bound alone decides.
No kernel may reach another device: no remote copies, remote signals or barrier semaphores. Data moves between devices by JAX's collectives and lax.ppermute only.
A program may use at most 64 MiB of HBM per device.

v0:
```python
import math

import jax
import jax.numpy as jnp
from jax import lax
from jax.sharding import PartitionSpec as P

HIGH = lax.Precision.HIGHEST


def extended(x, sides, width):
    edges = {}
    for axis, dim in sides:
        size, length = (lax.axis_size(axis), x.shape[dim])
        up = [(i, (i + 1) % size) for i in range(size - 1)]
        last = lax.slice_in_dim(x, length - width, length, axis=dim)
        leading = lax.slice_in_dim(x, 0, width, axis=dim)
        edges[dim] = (
            lax.ppermute(last, axis, up),
            lax.ppermute(leading, axis, [(b, a) for a, b in up]),
        )
    done = []
    for _, dim in sides:
        low, high = edges[dim]
        around = [(width, width) if d in done else (0, 0) for d in range(x.ndim)]
        x = jnp.concatenate([jnp.pad(low, around), x, jnp.pad(high, around)], axis=dim)
        done.append(dim)
    return x


def sent_together(arrays, axis, split_dim, concat_dim, along):
    both = jnp.concatenate(arrays, axis=along)
    result, at, gathered = (
        lax.all_to_all(both, axis, split_axis=split_dim, concat_axis=concat_dim, tiled=True),
        0,
        [],
    )
    for a in arrays:
        gathered.append(lax.slice_in_dim(result, at, at + a.shape[along], axis=along))
        at += a.shape[along]
    return tuple(gathered)


def neighbours(padded):
    beside_all = padded[:, 2:, 1:-1, 1:-1] + padded[:, :-2, 1:-1, 1:-1]
    beside_all = beside_all + padded[:, 1:-1, 2:, 1:-1] + padded[:, 1:-1, :-2, 1:-1]
    return beside_all + padded[:, 1:-1, 1:-1, 2:] + padded[:, 1:-1, 1:-1, :-2]


def diffuse(field, diffusion):
    padded = extended(field, (("gz", 1), ("gy", 2)), 1)
    padded = jnp.pad(padded, ((0, 0), (0, 0), (0, 0), (1, 1)))
    return field + diffusion[:, None, None, None] * (neighbours(padded) - 6.0 * field)


def group_size(block_count, per_block):
    return math.gcd(block_count, max(1, 512 // per_block))


def one_hots(voxel_group, highs, lanes):
    high_ids = jnp.arange(highs, dtype=jnp.int32)
    lane_ids = jnp.arange(lanes, dtype=jnp.int32)
    onehot_high = ((voxel_group // lanes)[..., None] == high_ids).astype(jnp.float32)
    onehot_low = ((voxel_group % lanes)[..., None] == lane_ids).astype(jnp.float32)
    return (onehot_high, onehot_low)


def block_sums(values, voxel, highs, lanes, combine, init):
    quantities, block_count, per_block = values.shape
    group = group_size(block_count, per_block)
    steps_count = block_count // group
    grouped_vals = values.reshape(quantities, steps_count, group, per_block).transpose(1, 0, 2, 3)
    grouped_vox = voxel.reshape(steps_count, group, per_block)

    def step(carry, item):
        vals_group, vox_group, step_id = item
        onehot_high, onehot_low = one_hots(vox_group, highs, lanes)
        weighted = vals_group[:, :, :, None] * onehot_low[None]
        part = jnp.einsum("gch,qgcl->gqhl", onehot_high, weighted, precision=HIGH)
        return (combine(carry, part, step_id * group, group), None)

    result, unused = lax.scan(
        step, init, (grouped_vals, grouped_vox, jnp.arange(steps_count, dtype=jnp.int32))
    )
    return result


def block_reads(table_for, voxel, substrates, highs, lanes):
    block_count, per_block = voxel.shape
    group = group_size(block_count, per_block)
    steps_count = block_count // group
    grouped_vox = voxel.reshape(steps_count, group, per_block)

    def step(carry, item):
        vox_group, step_id = item
        onehot_high, onehot_low = one_hots(vox_group, highs, lanes)
        table = table_for(step_id * group, group)
        picked = jnp.einsum("gch,shl->gscl", onehot_high, table, precision=HIGH)
        return (carry, jnp.sum(picked * onehot_low[:, None], axis=3))

    unused, reads = lax.scan(step, 0, (grouped_vox, jnp.arange(steps_count, dtype=jnp.int32)))
    return reads.transpose(2, 0, 1, 3).reshape(substrates, block_count, per_block)


def deposit(secrete, uptake, cell_voxel, block_dest, voxels, lanes):
    substrates = secrete.shape[0]
    blocks = block_dest.shape[0]
    per_block = secrete.shape[1] // blocks
    highs = voxels // lanes
    slab_count = lax.axis_size("gz")
    targets = block_dest[:, 0]
    voxel_blocks = cell_voxel.reshape(blocks, per_block)
    capacity = max(2, 3 * blocks // slab_count)
    block_ids = jnp.arange(blocks, dtype=jnp.int32)
    matches = targets[:, None] == targets[None, :]
    earlier = block_ids[None, :] < block_ids[:, None]
    slot_index = jnp.sum((matches & earlier).astype(jnp.int32), axis=1)
    position = targets * capacity + slot_index
    slots = slab_count * capacity
    placing = (jnp.arange(slots, dtype=jnp.int32)[:, None] == position[None, :]).astype(jnp.float32)
    send_release = jnp.einsum(
        "pb,sbc->spc", placing, secrete.reshape(substrates, blocks, per_block), precision=HIGH
    )
    send_uptake = jnp.einsum(
        "pb,sbc->spc", placing, uptake.reshape(substrates, blocks, per_block), precision=HIGH
    )
    send_index = jnp.dot(placing, voxel_blocks.astype(jnp.float32), precision=HIGH)
    send_index = send_index.astype(jnp.int32).reshape(1, slots, per_block)
    got_release, got_uptake, got_index = (
        *sent_together((send_release, send_uptake), "gz", 1, 1, 0),
        lax.all_to_all(send_index, "gz", split_axis=1, concat_axis=1, tiled=True),
    )
    slot_voxel = got_index.reshape(slots, per_block)
    stacked = jnp.concatenate([got_release, got_uptake], axis=0)

    def add_all(carry, part, first, count):
        return carry + jnp.sum(part, axis=0)

    init = jnp.zeros((2 * substrates, highs, lanes), jnp.float32)
    summed = block_sums(stacked, slot_voxel, highs, lanes, add_all, init).reshape(
        2 * substrates, voxels
    )
    source = summed[:substrates]
    uptake_sum = summed[substrates:]

    def reader(updated):
        table = updated.reshape(substrates, highs, lanes)
        looked_up = block_reads(lambda first, count: table, slot_voxel, substrates, highs, lanes)
        returned = lax.all_to_all(looked_up, "gz", split_axis=1, concat_axis=1, tiled=True)
        back = jnp.einsum("pb,spc->sbc", placing, returned, precision=HIGH)
        return back.reshape(substrates, blocks * per_block)

    return (source, uptake_sum, reader)


def shards(field, diffusion, secrete, uptake, cell_voxel, block_dest):
    substrates = field.shape[0]
    lanes = field.shape[3]
    voxels = field.shape[1] * field.shape[2] * lanes
    source, uptake_sum, reader = deposit(secrete, uptake, cell_voxel, block_dest, voxels, lanes)
    diffused = diffuse(field, diffusion).reshape(substrates, voxels)
    updated = (diffused + source) / (1.0 + uptake_sum)
    cell_conc = reader(updated)
    return (updated.reshape(field.shape), cell_conc)


def solution(mesh):
    in_specs = (
        P("sa", ("grp", "gz"), "gy", None),
        P("sa"),
        P("sa", ("grp", "gz", "gy")),
        P("sa", ("grp", "gz", "gy")),
        P(("grp", "gz", "gy")),
        P(("grp", "gz", "gy"), None),
    )
    out_specs = (P("sa", ("grp", "gz"), "gy", None), P("sa", ("grp", "gz", "gy")))
    return jax.shard_map(shards, mesh=mesh, in_specs=in_specs, out_specs=out_specs, check_vma=False)
```

profile of v0, /device:TPU:80, one launch (start us, length us, event | category | flops | bytes accessed | tf_op | source)
XLA Modules:
  0.0 175.4 jit_solution(2650769230239795237)
XLA Ops:
  2.2 1.2 convolution_bitcast_fusion
  3.4 1.2 convolution_bitcast_fusion.1
  5.6 43.8 %all-to-all-start = ((f32[8,96,128]{2,0,1:T(8,128)}), f32[8,96,128]{2,0,1:T(8,128)S(1)}, u32[]{:S(2)}, u32[]{:S(2)}) async-start(f32[8,96,128]{2,0,1:T(8,128)} %copy.14), calls=%async_computation | async-start | bytes 786432 | tf_op jit(solution)/shard_map/all_to_all | solution.py:34
  49.5 3.7 %collective-permute-start.1 = (f32[4,1,8,128]{3,2,1,0:T(8,128)S(1)}, f32[4,1,8,128]{3,2,1,0:T(8,128)S(1)}, u32[]{:S(2)}, u32[]{:S(2)}) collective-permute-start(f32[4,1,8,128]{3,2,1,0:T(8,128)S(1)} %get-tuple-element.156), channel_id=1, source_target_pairs={{0,16},{16,32},{32,48},{48,64},{64,80},{80,96},{96,112},{112,128},... | collective-permute-start | bytes 49160 | tf_op jit(solution)/shard_map/ppermute | solution.py:19
  53.1 1.3 collective-permute-start
  54.5 1.3 collective-permute-start.2
  55.8 4.6 %collective-permute-start.3 = (f32[4,4,1,128]{3,2,1,0:T(1,128)S(1)}, f32[4,4,1,128]{3,2,1,0:T(1,128)S(1)}, u32[]{:S(2)}, u32[]{:S(2)}) collective-permute-start(f32[4,4,1,128]{3,2,1,0:T(1,128)S(1)} %get-tuple-element.153), channel_id=1, source_target_pairs={{0,2},{2,4},{4,6},{6,8},{8,10},{10,12},{12,14},{1,3},{3,5},{5,7},{... | collective-permute-start | bytes 24584 | tf_op jit(solution)/shard_map/ppermute | solution.py:19
  62.3 11.3 %all-to-all-done = f32[8,96,128]{2,0,1:T(8,128)S(1)} async-done(((f32[8,96,128]{2,0,1:T(8,128)}), f32[8,96,128]{2,0,1:T(8,128)S(1)}, u32[]{:S(2)}, u32[]{:S(2)}) %all-to-all-start) | async-done | bytes 393248 | tf_op jit(solution)/shard_map/all_to_all | solution.py:34
  73.6 6.1 %all-to-all-start.1 = ((s32[1,96,128]{2,0,1:T(1,128)}), s32[1,96,128]{2,0,1:T(1,128)S(1)}, u32[]{:S(2)}, u32[]{:S(2)}) async-start(s32[1,96,128]{2,0,1:T(1,128)} %bitcast.14), calls=%async_computation.1 | async-start | bytes 98304 | tf_op jit(solution)/shard_map/all_to_all | solution.py:131
  80.1 12.0 %all-to-all-done.1 = s32[1,96,128]{2,0,1:T(1,128)S(1)} async-done(((s32[1,96,128]{2,0,1:T(1,128)}), s32[1,96,128]{2,0,1:T(1,128)S(1)}, u32[]{:S(2)}, u32[]{:S(2)}) %all-to-all-start.1) | async-done | bytes 49184 | tf_op jit(solution)/shard_map/all_to_all | solution.py:131
  92.1 31.3 %while.26 = (s32[]{:T(128)}, f32[8,32,128]{2,1,0:T(8,128)S(1)}, f32[24,8,4,128]{3,2,1,0:T(4,128)S(1)}, s32[24,4,128]{2,1,0:T(4,128)S(1)}, s32[]{:T(128)}, /*index=5*/s32[]{:T(128)}) while((s32[]{:T(128)}, f32[8,32,128]{2,1,0:T(8,128)S(1)}, f32[24,8,4,128]{3,2,1,0:T(4,128)S(1)}, s32[24,4,128]{2,1,0:T(4,128)S(1)}, s32[]{:T(128)}, ...), condition=%wide.region_2.3_spmd.clone, body=%wide.region_1.2_spmd.clone.sunk | while | flops 202073600 | bytes 845911 | solution.py:82
  92.3 1.1 fusion.66
  93.6 1.1 fusion.66
  96.2 1.1 fusion.66
  97.5 1.1 fusion.66
  98.8 1.1 fusion.66
  100.1 1.1 fusion.66
  102.7 1.1 fusion.66
  104.0 1.1 fusion.66
  105.3 1.1 fusion.66
  106.6 1.1 fusion.66
  109.2 1.1 fusion.66
  110.5 1.1 fusion.66
  111.8 1.1 fusion.66
  113.2 1.1 fusion.66
  115.8 1.1 fusion.66
  118.4 1.1 fusion.66
  119.7 1.1 fusion.66
  122.3 1.1 fusion.66
  123.5 31.9 %while.25 = (s32[]{:T(128)}, f32[24,4,4,128]{3,2,1,0:T(4,128)}, s32[24,4,128]{2,1,0:T(4,128)S(1)}, f32[4,32,128]{2,1,0:T(8,128)S(1)}, s32[]{:T(128)}) while((s32[]{:T(128)}, f32[24,4,4,128]{3,2,1,0:T(4,128)}, s32[24,4,128]{2,1,0:T(4,128)S(1)}, f32[4,32,128]{2,1,0:T(8,128)S(1)}, s32[]{:T(128)}) %tuple.72), condition=%wide.region_5.6_spmd, body=%wide.region_3.5_spmd.sunk | while | flops 101342720 | bytes 625217 | solution.py:101
  155.4 4.0 %all-to-all-start.2 = ((f32[4,96,128]{2,0,1:T(4,128)}), f32[4,96,128]{2,0,1:T(4,128)S(1)}, u32[]{:S(2)}, u32[]{:S(2)}) async-start(f32[4,96,128]{2,0,1:T(4,128)} %bitcast.20), calls=%async_computation.2 | async-start | bytes 393216 | tf_op jit(solution)/shard_map/all_to_all | solution.py:149
  160.0 14.5 %all-to-all-done.2 = f32[4,96,128]{2,0,1:T(4,128)S(1)} async-done(((f32[4,96,128]{2,0,1:T(4,128)}), f32[4,96,128]{2,0,1:T(4,128)S(1)}, u32[]{:S(2)}, u32[]{:S(2)}) %all-to-all-start.2) | async-done | bytes 196640 | tf_op jit(solution)/shard_map/all_to_all | solution.py:149
  (204 shorter events, 48.5 us)
Async XLA Ops:
  5.6 43.8 %copy-start = (f32[4,4,8,128]{3,2,1,0:T(8,128)S(1)}, f32[4,4,8,128]{3,2,1,0:T(8,128)}, u32[]{:S(2)}) copy-start(f32[4,4,8,128]{3,2,1,0:T(8,128)} %param.10) | copy-start | bytes 196612
  5.6 54.8 %copy-start.1 = (s32[4096]{0:T(1024)S(1)}, s32[4096]{0:T(1024)}, u32[]{:S(2)}) copy-start(s32[4096]{0:T(1024)} %param.14) | copy-start | bytes 49156
  5.6 68.0 %all-to-all-start = ((f32[8,96,128]{2,0,1:T(8,128)}), f32[8,96,128]{2,0,1:T(8,128)S(1)}, u32[]{:S(2)}, u32[]{:S(2)}) async-start(f32[8,96,128]{2,0,1:T(8,128)} %copy.14), calls=%async_computation | async-start | bytes 786432 | tf_op jit(solution)/shard_map/all_to_all | solution.py:34
  49.5 12.9 %collective-permute-start.1 = (f32[4,1,8,128]{3,2,1,0:T(8,128)S(1)}, f32[4,1,8,128]{3,2,1,0:T(8,128)S(1)}, u32[]{:S(2)}, u32[]{:S(2)}) collective-permute-start(f32[4,1,8,128]{3,2,1,0:T(8,128)S(1)} %get-tuple-element.156), channel_id=1, source_target_pairs={{0,16},{16,32},{32,48},{48,64},{64,80},{80,96},{96,112},{112,128},... | collective-permute-start | bytes 49160 | tf_op jit(solution)/shard_map/ppermute | solution.py:19
  53.1 26.6 %collective-permute-start = (f32[4,1,8,128]{3,2,1,0:T(8,128)S(1)}, f32[4,1,8,128]{3,2,1,0:T(8,128)S(1)}, u32[]{:S(2)}, u32[]{:S(2)}) collective-permute-start(f32[4,1,8,128]{3,2,1,0:T(8,128)S(1)} %get-tuple-element.155), channel_id=1, source_target_pairs={{16,0},{32,16},{48,32},{64,48},{80,64},{96,80},{112,96},{128,112},... | collective-permute-start | bytes 49160 | tf_op jit(solution)/shard_map/ppermute | solution.py:20
  54.5 6.9 %collective-permute-start.2 = (f32[4,4,1,128]{3,2,1,0:T(1,128)S(1)}, f32[4,4,1,128]{3,2,1,0:T(1,128)S(1)}, u32[]{:S(2)}, u32[]{:S(2)}) collective-permute-start(f32[4,4,1,128]{3,2,1,0:T(1,128)S(1)} %get-tuple-element.154), channel_id=1, source_target_pairs={{2,0},{4,2},{6,4},{8,6},{10,8},{12,10},{14,12},{3,1},{5,3},{7,5},{... | collective-permute-start | bytes 24584 | tf_op jit(solution)/shard_map/ppermute | solution.py:20
  55.8 5.9 %collective-permute-start.3 = (f32[4,4,1,128]{3,2,1,0:T(1,128)S(1)}, f32[4,4,1,128]{3,2,1,0:T(1,128)S(1)}, u32[]{:S(2)}, u32[]{:S(2)}) collective-permute-start(f32[4,4,1,128]{3,2,1,0:T(1,128)S(1)} %get-tuple-element.153), channel_id=1, source_target_pairs={{0,2},{2,4},{4,6},{6,8},{8,10},{10,12},{12,14},{1,3},{3,5},{5,7},{... | collective-permute-start | bytes 24584 | tf_op jit(solution)/shard_map/ppermute | solution.py:19
  73.6 18.5 %all-to-all-start.1 = ((s32[1,96,128]{2,0,1:T(1,128)}), s32[1,96,128]{2,0,1:T(1,128)S(1)}, u32[]{:S(2)}, u32[]{:S(2)}) async-start(s32[1,96,128]{2,0,1:T(1,128)} %bitcast.14), calls=%async_computation.1 | async-start | bytes 98304 | tf_op jit(solution)/shard_map/all_to_all | solution.py:131
  92.1 31.3 %copy-start.2 = (f32[4]{0:T(128)S(1)}, f32[4]{0:T(128)}, u32[]{:S(2)}) copy-start(f32[4]{0:T(128)} %param.11) | copy-start | bytes 52
  155.4 19.1 %all-to-all-start.2 = ((f32[4,96,128]{2,0,1:T(4,128)}), f32[4,96,128]{2,0,1:T(4,128)S(1)}, u32[]{:S(2)}, u32[]{:S(2)}) async-start(f32[4,96,128]{2,0,1:T(4,128)} %bitcast.20), calls=%async_computation.2 | async-start | bytes 393216 | tf_op jit(solution)/shard_map/all_to_all | solution.py:149
where the time goes:
time: 176 us; the launch traced here: 175 us
  starting transfers between devices  64.7 us (37%)
  matrix products  46.2 us (26%)
  waiting for transfers between devices  38.8 us (22%)
  local copies, waits for them, and re-layouts  16.4 us (9%)
  other arithmetic  7.01 us (4%)
    all_to_all x1, starting transfers between devices, sent_together(): lax.all_to_all(both, axis, split_axis=split_dim, concat_axis=concat_dim,...  43.8 us
    dot_general x24, matrix products, step(): part = jnp.einsum('gch,qgcl->gqhl', onehot_high, weighted, precision=HIGH)  26.3 us
    dot_general x24, matrix products, step(): picked = jnp.einsum('gch,shl->gscl', onehot_high, table, precision=HIGH)  16.4 us
    all_to_all x1, waiting for transfers between devices, reader(): lax.all_to_all(looked_up, 'gz', split_axis=1, concat_axis=1, tiled=True)  14.5 us
    dynamic_update_slice x24, local copies, waits for them, and re-layouts, block_reads(): lax.scan(step, 0, (grouped_vox, jnp.arange(steps_count, dtype=jnp.int32)))  14.4 us
    all_to_all x1, waiting for transfers between devices, deposit(): lax.all_to_all(send_index, 'gz', split_axis=1, concat_axis=1, tiled=True)  12 us
    all_to_all x1, waiting for transfers between devices, sent_together(): lax.all_to_all(both, axis, split_axis=split_dim, concat_axis=concat_dim,...  11.3 us
    ppermute x2, starting transfers between devices, extended(): lax.ppermute(last, axis, up)  8.24 us
  transfers between devices with their start and end apart: 7, of which 5 were waited for; matrix products, arithmetic and copies ran while one was open for 1% of the time, Pallas kernels for 0%

commit v1 on v0

v1 whole, which is shorter than its diff:
```python
import functools

import jax
import jax.numpy as jnp
from jax import lax
from jax.experimental import pallas as pl
from jax.experimental.pallas import tpu as pltpu
from jax.sharding import PartitionSpec as P

CAP = 6


def extended(x, sides, width):
    edges = {}
    for axis, dim in sides:
        size, length = (lax.axis_size(axis), x.shape[dim])
        up = [(i, (i + 1) % size) for i in range(size - 1)]
        last = lax.slice_in_dim(x, length - width, length, axis=dim)
        leading = lax.slice_in_dim(x, 0, width, axis=dim)
        edges[dim] = (
            lax.ppermute(last, axis, up),
            lax.ppermute(leading, axis, [(b, a) for a, b in up]),
        )
    done = []
    for _, dim in sides:
        low, high = edges[dim]
        around = [(width, width) if d in done else (0, 0) for d in range(x.ndim)]
        x = jnp.concatenate([jnp.pad(low, around), x, jnp.pad(high, around)], axis=dim)
        done.append(dim)
    return x


def neighbours(padded):
    beside_all = padded[:, 2:, 1:-1, 1:-1] + padded[:, :-2, 1:-1, 1:-1]
    beside_all = beside_all + padded[:, 1:-1, 2:, 1:-1] + padded[:, 1:-1, :-2, 1:-1]
    return beside_all + padded[:, 1:-1, 1:-1, 2:] + padded[:, 1:-1, 1:-1, :-2]


def diffuse(field, diffusion):
    padded = extended(field, (("gz", 1), ("gy", 2)), 1)
    padded = jnp.pad(padded, ((0, 0), (0, 0), (0, 0), (1, 1)))
    return field + diffusion[:, None, None, None] * (neighbours(padded) - 6.0 * field)


def rows_of(channels):
    return CAP * channels, -(-(CAP * channels + CAP) // 8) * 8


def pack_kernel(dest, secrete, uptake, voxel, out, used, *, blocks, cells, subs):
    slabs = out.shape[0]
    base, rows = rows_of(2 * subs)
    out[:, pl.ds(0, base), :] = jnp.zeros((slabs, base, cells), jnp.float32)
    out[:, pl.ds(base, rows - base), :] = jnp.full((slabs, rows - base, cells), -1.0, jnp.float32)
    for i in range(slabs):
        used[i] = 0
    for b in range(blocks):
        to = dest[b]
        slot = used[to]
        used[to] = slot + 1
        at = slice(b * cells, (b + 1) * cells)
        out[to, pl.ds(slot * 2 * subs, subs), :] = secrete[:, at]
        out[to, pl.ds(slot * 2 * subs + subs, subs), :] = uptake[:, at]
        out[to, pl.ds(base + slot, 1), :] = voxel[b : b + 1, :].astype(jnp.float32)


def place_kernel(dest, came, out, used, *, blocks, cells, subs):
    for i in range(came.shape[0]):
        used[i] = 0
    for b in range(blocks):
        to = dest[b]
        slot = used[to]
        used[to] = slot + 1
        out[:, b * cells : (b + 1) * cells] = came[to, pl.ds(slot * subs, subs), :]


def halves(x):
    high = x.astype(jnp.bfloat16)
    return high, (x - high.astype(jnp.float32)).astype(jnp.bfloat16)


def cells_of_pair(got, i, j, base, highs, lanes):
    v = jnp.concatenate(
        [got[i, pl.ds(base + 2 * j, 1), :], got[i, pl.ds(base + 2 * j + 1, 1), :]], axis=1
    ).astype(jnp.int32)
    row = v // lanes
    high = jnp.where(v < 0, -1, row % highs)
    low = v % lanes + lanes * (row // highs)
    wide = 2 * lanes
    mask = lax.broadcasted_iota(jnp.int32, (highs, wide), 0) == high
    lows = jnp.broadcast_to(low.astype(jnp.float32), (wide, wide)).astype(jnp.bfloat16)
    ids = lax.broadcasted_iota(jnp.int32, (wide, wide), 0).astype(jnp.float32).astype(jnp.bfloat16)
    one, zero = jnp.bfloat16(1.0), jnp.bfloat16(0.0)
    return mask, jnp.where(ids == lows, one, zero)


def cell_kernel(got, diffused, new_field, back, acc, table, *, subs):
    slabs, _, lanes = got.shape
    channels = 2 * subs
    base, _ = rows_of(channels)
    highs = diffused.shape[1] // 2
    wide = 2 * lanes
    pairs = CAP // 2
    acc[...] = jnp.zeros(acc.shape, jnp.float32)

    def add(i, unused):
        for j in range(pairs):
            mask, onehot = cells_of_pair(got, i, j, base, highs, lanes)
            two = [got[i, pl.ds((2 * j + k) * channels, channels), :] for k in range(2)]
            high, low = halves(jnp.concatenate(two, axis=1))
            values = jnp.concatenate([high.astype(jnp.float32), low.astype(jnp.float32)], axis=0)
            spread = jnp.where(mask[None], values[:, None, :], 0.0).astype(jnp.bfloat16)
            spread = spread.reshape(2 * channels * highs, wide)
            acc[...] += lax.dot_general(
                spread, onehot, (((1,), (1,)), ((), ())), preferred_element_type=jnp.float32
            )
        return unused

    lax.fori_loop(0, slabs, add, 0)
    half = channels * highs
    sums = (acc[0:half, :] + acc[half : 2 * half, :]).reshape(channels, highs, wide)
    sums = jnp.concatenate([sums[:, :, :lanes], sums[:, :, lanes:]], axis=1)
    new = (diffused[...] + sums[:subs]) / (1.0 + sums[subs:])
    new_field[...] = new
    by_low = jnp.concatenate([new[:, :highs], new[:, highs:]], axis=2).reshape(subs * highs, wide)
    part = halves(by_low)
    table[...] = jnp.concatenate(part, axis=0)

    def read(i, unused):
        for j in range(pairs):
            mask, onehot = cells_of_pair(got, i, j, base, highs, lanes)
            rows = jnp.dot(table[...], onehot, preferred_element_type=jnp.float32)
            rows = (rows[: subs * highs] + rows[subs * highs :]).reshape(subs, highs, wide)
            found = jnp.sum(jnp.where(mask[None], rows, 0.0), axis=1)
            for k in range(2):
                back[i, pl.ds((2 * j + k) * subs, subs), :] = found[:, k * lanes : (k + 1) * lanes]
        return unused

    lax.fori_loop(0, slabs, read, 0)


def small(mebibytes):
    return pltpu.CompilerParams(vmem_limit_bytes=mebibytes << 20)


def vmem():
    return pl.BlockSpec(memory_space=pltpu.VMEM)


def smem():
    return pl.BlockSpec(memory_space=pltpu.SMEM)


def shards(field, diffusion, secrete, uptake, cell_voxel, block_dest):
    subs, lanes = field.shape[0], field.shape[3]
    lines = field.shape[1] * field.shape[2]
    blocks = block_dest.shape[0]
    cells = secrete.shape[1] // blocks
    slabs = lax.axis_size("gz")
    base, rows = rows_of(2 * subs)
    f32 = functools.partial(jax.ShapeDtypeStruct, dtype=jnp.float32)
    dest = block_dest.reshape(blocks)
    sent = pl.pallas_call(
        functools.partial(pack_kernel, blocks=blocks, cells=cells, subs=subs),
        out_shape=f32((slabs, rows, cells)),
        in_specs=[smem(), vmem(), vmem(), vmem()],
        out_specs=vmem(),
        scratch_shapes=[pltpu.SMEM((slabs,), jnp.int32)],
        compiler_params=small(4),
        name="pack",
    )(dest, secrete, uptake, cell_voxel.reshape(blocks, cells))
    got = lax.all_to_all(sent, "gz", split_axis=0, concat_axis=0, tiled=True)
    diffused = diffuse(field, diffusion).reshape(subs, lines, lanes)
    new_field, back = pl.pallas_call(
        functools.partial(cell_kernel, subs=subs),
        out_shape=(f32((subs, lines, lanes)), f32((slabs, CAP * subs, cells))),
        in_specs=[vmem(), vmem()],
        out_specs=(vmem(), vmem()),
        scratch_shapes=[
            pltpu.VMEM((4 * subs * lines // 2, 2 * lanes), jnp.float32),
            pltpu.VMEM((2 * subs * lines // 2, 2 * lanes), jnp.bfloat16),
        ],
        compiler_params=small(8),
        name="cells",
    )(got, diffused)
    came = lax.all_to_all(back, "gz", split_axis=0, concat_axis=0, tiled=True)
    cell_conc = pl.pallas_call(
        functools.partial(place_kernel, blocks=blocks, cells=cells, subs=subs),
        out_shape=f32((subs, blocks * cells)),
        in_specs=[smem(), vmem()],
        out_specs=vmem(),
        scratch_shapes=[pltpu.SMEM((slabs,), jnp.int32)],
        compiler_params=small(4),
        name="place",
    )(dest, came)
    return (new_field.reshape(field.shape), cell_conc)


def solution(mesh):
    in_specs = (
        P("sa", ("grp", "gz"), "gy", None),
        P("sa"),
        P("sa", ("grp", "gz", "gy")),
        P("sa", ("grp", "gz", "gy")),
        P(("grp", "gz", "gy")),
        P(("grp", "gz", "gy"), None),
    )
    out_specs = (P("sa", ("grp", "gz"), "gy", None), P("sa", ("grp", "gz", "gy")))
    return jax.shard_map(shards, mesh=mesh, in_specs=in_specs, out_specs=out_specs, check_vma=False)
```

time: 176 us -> 111 us (0.63)
  matrix products: 46.2 us -> 0 us
  blocking collectives: 0 us -> 22.4 us
  waiting for transfers between devices: 38.8 us -> 16.7 us
  local copies, waits for them, and re-layouts: 16.4 us -> 3.47 us
  Pallas kernels: 0 us -> 12.8 us
  starting transfers between devices: 64.7 us -> 53.6 us
  other arithmetic: 7.01 us -> 0.37 us
    dot_general x52 -> x0, matrix products: 46.2 us -> none  [the longest x24 26.3 us: step(): part = jnp.einsum('gch,qgcl->gqhl', onehot_high, weighted, precision=HIGH)]
    all_to_all x3 -> x1, waiting for transfers between devices: 37.8 us -> 5.45 us  [shards(): got = lax.all_to_all(sent, 'gz', split_axis=0, concat_axis=0, tiled=True)]
    all_to_all x0 -> x1, blocking collectives: none -> 22.4 us  [shards(): came = lax.all_to_all(back, 'gz', split_axis=0, concat_axis=0, tiled=True)]
    dynamic_update_slice x24 -> x0, local copies, waits for them, and re-layouts: 14.4 us -> none  [block_reads(): lax.scan(step, 0, (grouped_vox, jnp.arange(steps_count, dtype=jnp.int32)))]
    pallas_call x0 -> x3, Pallas kernels: none -> 12.8 us  [the longest x1 10 us: shards(): pl.pallas_call(functools.partial(cell_kernel, subs=subs), out_shape=(f32(...]
    all_to_all x3 -> x1, starting transfers between devices: 53.8 us -> 43.8 us  [shards(): got = lax.all_to_all(sent, 'gz', split_axis=0, concat_axis=0, tiled=True)]
    ppermute x2, waiting for transfers between devices: 0.01 us -> 8.99 us  [extended(): lax.ppermute(leading, axis, [(b, a) for a, b in up])]
    convert_element_type x48 -> x0, other arithmetic: 3.76 us -> none  [one_hots(): ((voxel_group % lanes)[..., None] == lane_ids).astype(jnp.float32)]
  transfers between devices with their start and end apart: 7 -> 5, of which waited for: 5 -> 4; matrix products, arithmetic and copies ran while one was open for 1% -> 0% of each run, Pallas kernels for 0% -> 0%
where the time goes in v1:
time: 111 us; the launch traced here: 110 us
  starting transfers between devices  53.6 us (48%)
  blocking collectives  22.4 us (20%)
  waiting for transfers between devices  16.7 us (15%)
  Pallas kernels  12.8 us (12%)
  local copies, waits for them, and re-layouts  3.47 us (3%)
    all_to_all x1, starting transfers between devices, shards(): got = lax.all_to_all(sent, 'gz', split_axis=0, concat_axis=0, tiled=True)  43.8 us
    all_to_all x1, blocking collectives, shards(): came = lax.all_to_all(back, 'gz', split_axis=0, concat_axis=0, tiled=True)  22.4 us
    pallas_call x1, Pallas kernels, shards(): pl.pallas_call(functools.partial(cell_kernel, subs=subs), out_shape=(f32(...  10 us
    ppermute x2, waiting for transfers between devices, extended(): lax.ppermute(leading, axis, [(b, a) for a, b in up])  8.99 us
    ppermute x2, starting transfers between devices, extended(): lax.ppermute(last, axis, up)  7.21 us
    all_to_all x1, waiting for transfers between devices, shards(): got = lax.all_to_all(sent, 'gz', split_axis=0, concat_axis=0, tiled=True)  5.45 us
    unnamed x14, local copies, waits for them, and re-layouts  3.43 us
    ppermute x2, starting transfers between devices, extended(): lax.ppermute(leading, axis, [(b, a) for a, b in up])  2.62 us
  transfers between devices with their start and end apart: 5, of which 4 were waited for; matrix products, arithmetic and copies ran while one was open for 0% of the time, Pallas kernels for 0%

profile of v1, /device:TPU:80, one launch (start us, length us, event | category | flops | bytes accessed | tf_op | source)
XLA Modules:
  0.0 110.1 jit_solution(16471954659748376074)
XLA Ops:
  0.6 0.0 copy-start.3
  0.6 0.6 copy-done.3
  1.3 0.0 copy-start
  1.3 0.8 copy-done
  2.1 0.0 copy-start.1
  2.1 0.8 copy-done.1
  3.0 0.0 copy-start.2
  3.0 0.7 copy-done.2
  3.7 1.5 %pack.1 = f32[16,56,128]{2,1,0:T(8,128)} custom-call(s32[32]{0:T(128)S(1)} %bitcast.6, f32[4,4096]{1,0:T(4,128)S(1)} %copy-done, f32[4,4096]{1,0:T(4,128)S(1)} %copy-done.1, s32[32,128]{1,0:T(8,128)S(1)} %bitcast.5), custom_call_target="tpu_custom_call" | custom-call | tf_op jit(solution)/shard_map/pack/pallas_call | solution.py:162
  5.2 0.0 copy-start.4
  5.2 43.8 %all-to-all-start = ((f32[16,56,128]{2,1,0:T(8,128)}), f32[16,56,128]{2,1,0:T(8,128)S(1)}, u32[]{:S(2)}, u32[]{:S(2)}) async-start(f32[16,56,128]{2,1,0:T(8,128)} %pack.1), calls=%async_computation | async-start | bytes 917504 | tf_op jit(solution)/shard_map/all_to_all | solution.py:171
  49.0 0.0 copy-done.4
  49.0 3.7 %collective-permute-start.1 = (f32[4,1,8,128]{3,2,1,0:T(8,128)S(1)}, f32[4,1,8,128]{3,2,1,0:T(8,128)S(1)}, u32[]{:S(2)}, u32[]{:S(2)}) collective-permute-start(f32[4,1,8,128]{3,2,1,0:T(8,128)S(1)} %get-tuple-element.9), channel_id=1, source_target_pairs={{0,16},{16,32},{32,48},{48,64},{64,80},{80,96},{96,112},{112,128},... | collective-permute-start | bytes 49160 | tf_op jit(solution)/shard_map/ppermute | solution.py:21
  52.7 3.6 %collective-permute-start.3 = (f32[4,4,1,128]{3,2,1,0:T(1,128)S(1)}, f32[4,4,1,128]{3,2,1,0:T(1,128)S(1)}, u32[]{:S(2)}, u32[]{:S(2)}) collective-permute-start(f32[4,4,1,128]{3,2,1,0:T(1,128)S(1)} %get-tuple-element.6), channel_id=1, source_target_pairs={{0,2},{2,4},{4,6},{6,8},{8,10},{10,12},{12,14},{1,3},{3,5},{5,7},{... | collective-permute-start | bytes 24584 | tf_op jit(solution)/shard_map/ppermute | solution.py:21
  56.2 1.3 %collective-permute-start.2 = (f32[4,4,1,128]{3,2,1,0:T(1,128)S(1)}, f32[4,4,1,128]{3,2,1,0:T(1,128)S(1)}, u32[]{:S(2)}, u32[]{:S(2)}) collective-permute-start(f32[4,4,1,128]{3,2,1,0:T(1,128)S(1)} %get-tuple-element.7), channel_id=1, source_target_pairs={{2,0},{4,2},{6,4},{8,6},{10,8},{12,10},{14,12},{3,1},{5,3},{7,5},{... | collective-permute-start | bytes 24584 | tf_op jit(solution)/shard_map/ppermute | solution.py:22
  57.6 1.3 %collective-permute-start = (f32[4,1,8,128]{3,2,1,0:T(8,128)S(1)}, f32[4,1,8,128]{3,2,1,0:T(8,128)S(1)}, u32[]{:S(2)}, u32[]{:S(2)}) collective-permute-start(f32[4,1,8,128]{3,2,1,0:T(8,128)S(1)} %get-tuple-element.8), channel_id=1, source_target_pairs={{16,0},{32,16},{48,32},{64,48},{80,64},{96,80},{112,96},{128,112},... | collective-permute-start | bytes 49160 | tf_op jit(solution)/shard_map/ppermute | solution.py:22
  58.9 0.0 collective-permute-done.3
  58.9 2.9 %collective-permute-done.2 = f32[4,4,1,128]{3,2,1,0:T(1,128)S(1)} collective-permute-done((f32[4,4,1,128]{3,2,1,0:T(1,128)S(1)}, f32[4,4,1,128]{3,2,1,0:T(1,128)S(1)}, u32[]{:S(2)}, u32[]{:S(2)}) %collective-permute-start.2) | collective-permute-done | bytes 8224 | tf_op jit(solution)/shard_map/ppermute | solution.py:22
  61.8 2.2 %collective-permute-done.1 = f32[4,1,8,128]{3,2,1,0:T(8,128)S(1)} collective-permute-done((f32[4,1,8,128]{3,2,1,0:T(8,128)S(1)}, f32[4,1,8,128]{3,2,1,0:T(8,128)S(1)}, u32[]{:S(2)}, u32[]{:S(2)}) %collective-permute-start.1) | collective-permute-done | bytes 16416 | tf_op jit(solution)/shard_map/ppermute | solution.py:21
  64.1 6.1 %collective-permute-done = f32[4,1,8,128]{3,2,1,0:T(8,128)S(1)} collective-permute-done((f32[4,1,8,128]{3,2,1,0:T(8,128)S(1)}, f32[4,1,8,128]{3,2,1,0:T(8,128)S(1)}, u32[]{:S(2)}, u32[]{:S(2)}) %collective-permute-start) | collective-permute-done | bytes 16416 | tf_op jit(solution)/shard_map/ppermute | solution.py:22
  70.2 0.0 copy-start.5
  70.2 0.3 select_maximum_fusion
  70.4 0.4 copy-done.5
  70.8 0.1 fusion.4.diffused
  70.9 5.5 %all-to-all-done.got = f32[16,56,128]{2,1,0:T(8,128)S(1)} async-done(((f32[16,56,128]{2,1,0:T(8,128)}), f32[16,56,128]{2,1,0:T(8,128)S(1)}, u32[]{:S(2)}, u32[]{:S(2)}) %all-to-all-start) | async-done | bytes 458784 | tf_op jit(solution)/shard_map/all_to_all | solution.py:171
  76.4 10.0 %cells.1 = (f32[4,32,128]{2,1,0:T(8,128)}, f32[16,24,128]{2,1,0:T(8,128)S(1)}) custom-call(f32[16,56,128]{2,1,0:T(8,128)S(1)} %all-to-all-done.got, f32[4,32,128]{2,1,0:T(8,128)S(1)} %fusion.4.diffused), custom_call_target="tpu_custom_call" | custom-call | tf_op jit(solution)/shard_map/cells/pallas_call | solution.py:173
  86.4 22.4 %all_to_all.10.came = f32[16,24,128]{2,1,0:T(8,128)S(1)} all-to-all(f32[16,24,128]{2,1,0:T(8,128)S(1)} %get-tuple-element.5), channel_id=1, replica_groups=mesh['grp'=2,'gz'=16,'gy'=8,'sa'=2] {'gz'}, dimensions={0} | all-to-all | bytes 393216 | tf_op jit(solution)/shard_map/all_to_all | solution.py:185
  108.8 1.3 %place.1 = f32[4,4096]{1,0:T(4,128)} custom-call(s32[32]{0:T(128)S(1)} %bitcast.7, f32[16,24,128]{2,1,0:T(8,128)S(1)} %all_to_all.10.came), custom_call_target="tpu_custom_call" | custom-call | tf_op jit(solution)/shard_map/place/pallas_call | solution.py:186
  (7 shorter events, 0.0 us)
Async XLA Ops:
  0.6 0.7 copy-start.3
  1.3 0.8 copy-start
  2.1 0.8 copy-start.1
  3.0 0.7 copy-start.2
  5.2 43.8 %copy-start.4 = (f32[4,4,8,128]{3,2,1,0:T(8,128)S(1)}, f32[4,4,8,128]{3,2,1,0:T(8,128)}, u32[]{:S(2)}) copy-start(f32[4,4,8,128]{3,2,1,0:T(8,128)} %param.6) | copy-start | bytes 196612
  5.2 71.2 %all-to-all-start = ((f32[16,56,128]{2,1,0:T(8,128)}), f32[16,56,128]{2,1,0:T(8,128)S(1)}, u32[]{:S(2)}, u32[]{:S(2)}) async-start(f32[16,56,128]{2,1,0:T(8,128)} %pack.1), calls=%async_computation | async-start | bytes 917504 | tf_op jit(solution)/shard_map/all_to_all | solution.py:171
  49.0 15.1 %collective-permute-start.1 = (f32[4,1,8,128]{3,2,1,0:T(8,128)S(1)}, f32[4,1,8,128]{3,2,1,0:T(8,128)S(1)}, u32[]{:S(2)}, u32[]{:S(2)}) collective-permute-start(f32[4,1,8,128]{3,2,1,0:T(8,128)S(1)} %get-tuple-element.9), channel_id=1, source_target_pairs={{0,16},{16,32},{32,48},{48,64},{64,80},{80,96},{96,112},{112,128},... | collective-permute-start | bytes 49160 | tf_op jit(solution)/shard_map/ppermute | solution.py:21
  52.7 6.2 %collective-permute-start.3 = (f32[4,4,1,128]{3,2,1,0:T(1,128)S(1)}, f32[4,4,1,128]{3,2,1,0:T(1,128)S(1)}, u32[]{:S(2)}, u32[]{:S(2)}) collective-permute-start(f32[4,4,1,128]{3,2,1,0:T(1,128)S(1)} %get-tuple-element.6), channel_id=1, source_target_pairs={{0,2},{2,4},{4,6},{6,8},{8,10},{10,12},{12,14},{1,3},{3,5},{5,7},{... | collective-permute-start | bytes 24584 | tf_op jit(solution)/shard_map/ppermute | solution.py:21
  56.2 5.6 %collective-permute-start.2 = (f32[4,4,1,128]{3,2,1,0:T(1,128)S(1)}, f32[4,4,1,128]{3,2,1,0:T(1,128)S(1)}, u32[]{:S(2)}, u32[]{:S(2)}) collective-permute-start(f32[4,4,1,128]{3,2,1,0:T(1,128)S(1)} %get-tuple-element.7), channel_id=1, source_target_pairs={{2,0},{4,2},{6,4},{8,6},{10,8},{12,10},{14,12},{3,1},{5,3},{7,5},{... | collective-permute-start | bytes 24584 | tf_op jit(solution)/shard_map/ppermute | solution.py:22
  57.6 12.6 %collective-permute-start = (f32[4,1,8,128]{3,2,1,0:T(8,128)S(1)}, f32[4,1,8,128]{3,2,1,0:T(8,128)S(1)}, u32[]{:S(2)}, u32[]{:S(2)}) collective-permute-start(f32[4,1,8,128]{3,2,1,0:T(8,128)S(1)} %get-tuple-element.8), channel_id=1, source_target_pairs={{16,0},{32,16},{48,32},{64,48},{80,64},{96,80},{112,96},{128,112},... | collective-permute-start | bytes 49160 | tf_op jit(solution)/shard_map/ppermute | solution.py:22
  70.2 0.7 copy-start.5

commit v2 on v1

v2 whole, which is shorter than its diff:
```python
import functools

import jax
import jax.numpy as jnp
from jax import lax
from jax.experimental import pallas as pl
from jax.experimental.pallas import tpu as pltpu
from jax.sharding import PartitionSpec as P

CAP = 6


def extended(x, sides, width):
    edges = {}
    for axis, dim in sides:
        size, length = (lax.axis_size(axis), x.shape[dim])
        up = [(i, (i + 1) % size) for i in range(size - 1)]
        last = lax.slice_in_dim(x, length - width, length, axis=dim)
        leading = lax.slice_in_dim(x, 0, width, axis=dim)
        edges[dim] = (
            lax.ppermute(last, axis, up),
            lax.ppermute(leading, axis, [(b, a) for a, b in up]),
        )
    done = []
    for _, dim in sides:
        low, high = edges[dim]
        around = [(width, width) if d in done else (0, 0) for d in range(x.ndim)]
        x = jnp.concatenate([jnp.pad(low, around), x, jnp.pad(high, around)], axis=dim)
        done.append(dim)
    return x


def neighbours(padded):
    beside_all = padded[:, 2:, 1:-1, 1:-1] + padded[:, :-2, 1:-1, 1:-1]
    beside_all = beside_all + padded[:, 1:-1, 2:, 1:-1] + padded[:, 1:-1, :-2, 1:-1]
    return beside_all + padded[:, 1:-1, 1:-1, 2:] + padded[:, 1:-1, 1:-1, :-2]


def diffuse(field, diffusion):
    padded = extended(field, (("gz", 1), ("gy", 2)), 1)
    padded = jnp.pad(padded, ((0, 0), (0, 0), (0, 0), (1, 1)))
    return field + diffusion[:, None, None, None] * (neighbours(padded) - 6.0 * field)


def rows_of(channels):
    return CAP * channels, -(-(CAP * channels + CAP) // 8) * 8


def pack_kernel(
    dest_in, secrete_in, uptake_in, voxel_in, out, dest, secrete, uptake, voxel, used, sems, *, subs
):
    pairs = ((dest_in, dest), (secrete_in, secrete), (uptake_in, uptake), (voxel_in, voxel))
    copies = [pltpu.make_async_copy(a, b, sems.at[i]) for i, (a, b) in enumerate(pairs)]
    for copy in copies:
        copy.start()
    slabs, _, cells = out.shape
    base, rows = rows_of(2 * subs)
    out[:, pl.ds(base, rows - base), :] = jnp.full((slabs, rows - base, cells), -1.0, jnp.float32)
    for i in range(slabs):
        used[i] = 0
    for copy in copies:
        copy.wait()
    for b in range(dest.shape[0]):
        to = dest[b]
        slot = used[to]
        used[to] = slot + 1
        at = slice(b * cells, (b + 1) * cells)
        out[to, pl.ds(slot * 2 * subs, subs), :] = secrete[:, at]
        out[to, pl.ds(slot * 2 * subs + subs, subs), :] = uptake[:, at]
        out[to, pl.ds(base + slot, 1), :] = voxel[b : b + 1, :].astype(jnp.float32)
    for i in range(slabs):
        out[i, base + CAP : base + CAP + 1, :] = jnp.full((1, cells), used[i]).astype(jnp.float32)


def place_kernel(dest, came, out, used, *, blocks, cells, subs):
    for i in range(came.shape[0]):
        used[i] = 0
    for b in range(blocks):
        to = dest[b]
        slot = used[to]
        used[to] = slot + 1
        out[:, b * cells : (b + 1) * cells] = came[to, pl.ds(slot * subs, subs), :]


def halves(x):
    high = x.astype(jnp.bfloat16)
    return high, (x - high.astype(jnp.float32)).astype(jnp.bfloat16)


GROUP = 4
BITS = 10


def list_blocks(got, work, slabs, subs):
    base, rows = rows_of(2 * subs)
    counts = jnp.concatenate([got[i * rows + base + CAP : i * rows + base + CAP + 1, :] for i in range(slabs)], axis=0)
    lane = lax.broadcasted_iota(jnp.int32, (8, counts.shape[1]), 1)
    digit = lax.broadcasted_iota(jnp.int32, (8, counts.shape[1]), 0)
    scale = jnp.where(lane == 0, 1 << (3 * digit), 0).astype(jnp.float32)
    words = [jnp.sum(counts[8 * w : 8 * w + 8] * scale).astype(jnp.int32) for w in range(slabs // 8)]
    total, hole = jnp.int32(0), jnp.int32(0)
    for i in range(slabs):
        count = (words[i // 8] >> (3 * (i % 8))) & 7
        for slot in range(CAP):
            at = i * rows + slot * 2 * subs, i * rows + base + slot, i * CAP * subs + slot * subs
            code = at[0] | at[1] << BITS | at[2] << 2 * BITS
            work[total] = code
            taken = slot < count
            hole = jnp.where(taken, hole, code)
            total = total + taken.astype(jnp.int32)
    for k in range(GROUP - 1):
        work[total + k] = hole
    return total


def group_of(got, work, ids, g, highs, lanes):
    codes = [work[g * GROUP + k] for k in range(GROUP)]
    mask = (1 << BITS) - 1
    v = [got[pl.ds((c >> BITS) & mask, 1), :].astype(jnp.int32) for c in codes]
    v = jnp.concatenate(v, axis=1)
    row = v // lanes
    high = jnp.where(v < 0, -1, row % highs)
    low = v % lanes + lanes * (row // highs)
    many = GROUP * lanes
    here = lax.broadcasted_iota(jnp.int32, (highs, many), 0) == high
    lows = jnp.broadcast_to(low.astype(jnp.float32), (16, many)).astype(jnp.bfloat16)
    one, zero = jnp.bfloat16(1.0), jnp.bfloat16(0.0)
    tiles = []
    for t in range(2 * lanes // 16):
        own = jnp.concatenate([ids[t * 16 : t * 16 + 16, :]] * GROUP, axis=1)
        tiles.append(jnp.where(own == lows, one, zero))
    return codes, here, jnp.concatenate(tiles, axis=0)


def cell_kernel(got, diffused, sums_out, back, acc, table, ids, work, *, slabs, subs):
    lanes = got.shape[1]
    channels = 2 * subs
    highs = diffused.shape[1] // 2
    wide = 2 * lanes
    mask = (1 << BITS) - 1
    total = list_blocks(got, work, slabs, subs)
    steps = (total + GROUP - 1) // GROUP
    acc[...] = jnp.zeros(acc.shape, jnp.float32)
    ids[...] = lax.broadcasted_iota(jnp.int32, ids.shape, 0).astype(jnp.float32).astype(jnp.bfloat16)

    def add(g, unused):
        codes, here, onehot = group_of(got, work, ids, g, highs, lanes)
        own = [got[pl.ds(pl.multiple_of(c & mask, 8), channels), :] for c in codes]
        high, low = halves(jnp.concatenate(own, axis=1))
        values = jnp.concatenate([high.astype(jnp.float32), low.astype(jnp.float32)], axis=0)
        spread = jnp.where(here[None], values[:, None, :], 0.0).astype(jnp.bfloat16)
        spread = spread.reshape(2 * channels * highs, GROUP * lanes)
        acc[...] += lax.dot_general(
            spread, onehot, (((1,), (1,)), ((), ())), preferred_element_type=jnp.float32
        )
        return unused

    lax.fori_loop(0, steps, add, 0)
    half = channels * highs
    sums = (acc[0:half, :] + acc[half : 2 * half, :]).reshape(channels, highs, wide)
    sums = jnp.concatenate([sums[:, :, :lanes], sums[:, :, lanes:]], axis=1)
    sums_out[...] = sums
    new = (diffused[...] + sums[:subs]) / (1.0 + sums[subs:])
    by_low = jnp.concatenate([new[:, :highs], new[:, highs:]], axis=2).reshape(subs * highs, wide)
    table[...] = jnp.concatenate(halves(by_low), axis=0)

    def read(g, unused):
        codes, here, onehot = group_of(got, work, ids, g, highs, lanes)
        rows = jnp.dot(table[...], onehot, preferred_element_type=jnp.float32)
        rows = (rows[: subs * highs] + rows[subs * highs :]).reshape(subs, highs, GROUP * lanes)
        found = jnp.sum(jnp.where(here[None], rows, 0.0), axis=1)
        for k, c in enumerate(codes):
            back[pl.ds(c >> 2 * BITS, subs), :] = found[:, k * lanes : (k + 1) * lanes]
        return unused

    lax.fori_loop(0, steps, read, 0)


def small(mebibytes):
    return pltpu.CompilerParams(vmem_limit_bytes=mebibytes << 20)


def vmem():
    return pl.BlockSpec(memory_space=pltpu.VMEM)


def smem():
    return pl.BlockSpec(memory_space=pltpu.SMEM)


def shards(field, diffusion, secrete, uptake, cell_voxel, block_dest):
    subs, lanes = field.shape[0], field.shape[3]
    lines = field.shape[1] * field.shape[2]
    blocks = block_dest.shape[0]
    cells = secrete.shape[1] // blocks
    slabs = lax.axis_size("gz")
    base, rows = rows_of(2 * subs)
    f32 = functools.partial(jax.ShapeDtypeStruct, dtype=jnp.float32)
    dest = block_dest.reshape(blocks)
    sent = pl.pallas_call(
        functools.partial(pack_kernel, subs=subs),
        out_shape=f32((slabs, rows, cells)),
        in_specs=[pl.BlockSpec(memory_space=pltpu.HBM)] * 4,
        out_specs=vmem(),
        scratch_shapes=[
            pltpu.SMEM((blocks,), jnp.int32),
            pltpu.VMEM((subs, blocks * cells), jnp.float32),
            pltpu.VMEM((subs, blocks * cells), jnp.float32),
            pltpu.VMEM((blocks, cells), jnp.int32),
            pltpu.SMEM((slabs,), jnp.int32),
            pltpu.SemaphoreType.DMA((4,)),
        ],
        name="pack",
    )(dest, secrete, uptake, cell_voxel.reshape(blocks, cells))
    got = lax.all_to_all(sent, "gz", split_axis=0, concat_axis=0, tiled=True)
    diffused = diffuse(field, diffusion).reshape(subs, lines, lanes)
    sums, back = pl.pallas_call(
        functools.partial(cell_kernel, slabs=slabs, subs=subs),
        out_shape=(f32((2 * subs, lines, lanes)), f32((slabs * CAP * subs, cells))),
        in_specs=[vmem(), vmem()],
        out_specs=(vmem(), vmem()),
        scratch_shapes=[
            pltpu.VMEM((4 * subs * lines // 2, 2 * lanes), jnp.float32),
            pltpu.VMEM((2 * subs * lines // 2, 2 * lanes), jnp.bfloat16),
            pltpu.VMEM((2 * lanes, lanes), jnp.bfloat16),
            pltpu.SMEM((slabs * CAP + GROUP,), jnp.int32),
        ],
        compiler_params=small(8),
        name="cells",
    )(got.reshape(slabs * rows, cells), diffused)
    back = back.reshape(slabs, CAP * subs, cells)
    came = lax.all_to_all(back, "gz", split_axis=0, concat_axis=0, tiled=True)
    cell_conc = pl.pallas_call(
        functools.partial(place_kernel, blocks=blocks, cells=cells, subs=subs),
        out_shape=f32((subs, blocks * cells)),
        in_specs=[smem(), vmem()],
        out_specs=vmem(),
        scratch_shapes=[pltpu.SMEM((slabs,), jnp.int32)],
        compiler_params=small(4),
        name="place",
    )(dest, came)
    new_field = (diffused + sums[:subs]) / (1.0 + sums[subs:])
    return (new_field.reshape(field.shape), cell_conc)


def solution(mesh):
    in_specs = (
        P("sa", ("grp", "gz"), "gy", None),
        P("sa"),
        P("sa", ("grp", "gz", "gy")),
        P("sa", ("grp", "gz", "gy")),
        P(("grp", "gz", "gy")),
        P(("grp", "gz", "gy"), None),
    )
    out_specs = (P("sa", ("grp", "gz"), "gy", None), P("sa", ("grp", "gz", "gy")))
    return jax.shard_map(shards, mesh=mesh, in_specs=in_specs, out_specs=out_specs, check_vma=False)
```

time: 111 us -> 108 us (0.973)
  blocking collectives: 22.4 us -> 0 us
  waiting for transfers between devices: 16.7 us -> 29.8 us
  starting transfers between devices: 53.6 us -> 64.6 us
  local copies, waits for them, and re-layouts: 3.47 us -> 0.44 us
  Pallas kernels: 12.8 us -> 10.7 us
    all_to_all x1 -> x0, blocking collectives: 22.4 us -> none  [shards(): came = lax.all_to_all(back, 'gz', split_axis=0, concat_axis=0, tiled=True)]
    all_to_all x0 -> x1, waiting for transfers between devices: none -> 13.1 us  [shards(): came = lax.all_to_all(back, 'gz', split_axis=0, concat_axis=0, tiled=True)]
    all_to_all x0 -> x1, starting transfers between devices: none -> 10.9 us  [shards(): came = lax.all_to_all(back, 'gz', split_axis=0, concat_axis=0, tiled=True)]
    unnamed x14 -> x8, local copies, waits for them, and re-layouts: 3.43 us -> 0.4 us
    pallas_call x2, Pallas kernels: 11.5 us -> 9.36 us  [the longest x1 7.52 us: shards(): pl.pallas_call(functools.partial(cell_kernel, slabs=slabs, subs=subs), ou...]
  transfers between devices with their start and end apart: 5 -> 6, of which waited for: 4 -> 5; matrix products, arithmetic and copies ran while one was open for 0% -> 1% of each run, Pallas kernels for 0% -> 0%
where the time goes in v2:
time: 108 us; the launch traced here: 107 us
  starting transfers between devices  64.6 us (60%)
  waiting for transfers between devices  29.8 us (28%)
  Pallas kernels  10.7 us (10%)
    all_to_all x1, starting transfers between devices, shards(): got = lax.all_to_all(sent, 'gz', split_axis=0, concat_axis=0, tiled=True)  43.8 us
    all_to_all x1, waiting for transfers between devices, shards(): came = lax.all_to_all(back, 'gz', split_axis=0, concat_axis=0, tiled=True)  13.1 us
    all_to_all x1, starting transfers between devices, shards(): came = lax.all_to_all(back, 'gz', split_axis=0, concat_axis=0, tiled=True)  10.9 us
    ppermute x2, waiting for transfers between devices, extended(): lax.ppermute(leading, axis, [(b, a) for a, b in up])  8.99 us
    pallas_call x1, Pallas kernels, shards(): pl.pallas_call(functools.partial(cell_kernel, slabs=slabs, subs=subs), ou...  7.52 us
    ppermute x2, starting transfers between devices, extended(): lax.ppermute(last, axis, up)  7.21 us
    all_to_all x1, waiting for transfers between devices, shards(): got = lax.all_to_all(sent, 'gz', split_axis=0, concat_axis=0, tiled=True)  5.45 us
    ppermute x2, starting transfers between devices, extended(): lax.ppermute(leading, axis, [(b, a) for a, b in up])  2.62 us
  transfers between devices with their start and end apart: 6, of which 5 were waited for; matrix products, arithmetic and copies ran while one was open for 1% of the time, Pallas kernels for 0%

profile of v2, /device:TPU:80, one launch (start us, length us, event | category | flops | bytes accessed | tf_op | source)
XLA Modules:
  0.0 107.2 jit_solution(4651822352471003261)
XLA Ops:
  0.6 1.8 %pack.1 = f32[16,56,128]{2,1,0:T(8,128)} custom-call(s32[32]{0:T(128)} %bitcast.9, f32[4,4096]{1,0:T(4,128)} %secrete_in.1, f32[4,4096]{1,0:T(4,128)} %uptake_in.1, s32[32,128]{1,0:T(8,128)} %bitcast.11), custom_call_target="tpu_custom_call" | custom-call | tf_op jit(solution)/shard_map/pack/pallas_call | solution.py:200
  2.5 0.0 copy-start.1
  2.5 43.8 %all-to-all-start = ((f32[16,56,128]{2,1,0:T(8,128)}), f32[16,56,128]{2,1,0:T(8,128)S(1)}, u32[]{:S(2)}, u32[]{:S(2)}) async-start(f32[16,56,128]{2,1,0:T(8,128)} %pack.1), calls=%async_computation | async-start | bytes 917504 | tf_op jit(solution)/shard_map/all_to_all | solution.py:215
  46.3 0.0 copy-done.1
  46.3 3.7 %collective-permute-start.1 = (f32[4,1,8,128]{3,2,1,0:T(8,128)S(1)}, f32[4,1,8,128]{3,2,1,0:T(8,128)S(1)}, u32[]{:S(2)}, u32[]{:S(2)}) collective-permute-start(f32[4,1,8,128]{3,2,1,0:T(8,128)S(1)} %get-tuple-element.9), channel_id=1, source_target_pairs={{0,16},{16,32},{32,48},{48,64},{64,80},{80,96},{96,112},{112,128},... | collective-permute-start | bytes 49160 | tf_op jit(solution)/shard_map/ppermute | solution.py:21
  50.0 3.6 %collective-permute-start.3 = (f32[4,4,1,128]{3,2,1,0:T(1,128)S(1)}, f32[4,4,1,128]{3,2,1,0:T(1,128)S(1)}, u32[]{:S(2)}, u32[]{:S(2)}) collective-permute-start(f32[4,4,1,128]{3,2,1,0:T(1,128)S(1)} %get-tuple-element.6), channel_id=1, source_target_pairs={{0,2},{2,4},{4,6},{6,8},{8,10},{10,12},{12,14},{1,3},{3,5},{5,7},{... | collective-permute-start | bytes 24584 | tf_op jit(solution)/shard_map/ppermute | solution.py:21
  53.6 1.3 %collective-permute-start.2 = (f32[4,4,1,128]{3,2,1,0:T(1,128)S(1)}, f32[4,4,1,128]{3,2,1,0:T(1,128)S(1)}, u32[]{:S(2)}, u32[]{:S(2)}) collective-permute-start(f32[4,4,1,128]{3,2,1,0:T(1,128)S(1)} %get-tuple-element.7), channel_id=1, source_target_pairs={{2,0},{4,2},{6,4},{8,6},{10,8},{12,10},{14,12},{3,1},{5,3},{7,5},{... | collective-permute-start | bytes 24584 | tf_op jit(solution)/shard_map/ppermute | solution.py:22
  54.9 1.3 %collective-permute-start = (f32[4,1,8,128]{3,2,1,0:T(8,128)S(1)}, f32[4,1,8,128]{3,2,1,0:T(8,128)S(1)}, u32[]{:S(2)}, u32[]{:S(2)}) collective-permute-start(f32[4,1,8,128]{3,2,1,0:T(8,128)S(1)} %get-tuple-element.8), channel_id=1, source_target_pairs={{16,0},{32,16},{48,32},{64,48},{80,64},{96,80},{112,96},{128,112},... | collective-permute-start | bytes 49160 | tf_op jit(solution)/shard_map/ppermute | solution.py:22
  56.2 0.0 collective-permute-done.3
  56.3 2.9 %collective-permute-done.2 = f32[4,4,1,128]{3,2,1,0:T(1,128)S(1)} collective-permute-done((f32[4,4,1,128]{3,2,1,0:T(1,128)S(1)}, f32[4,4,1,128]{3,2,1,0:T(1,128)S(1)}, u32[]{:S(2)}, u32[]{:S(2)}) %collective-permute-start.2) | collective-permute-done | bytes 8224 | tf_op jit(solution)/shard_map/ppermute | solution.py:22
  59.2 2.2 %collective-permute-done.1 = f32[4,1,8,128]{3,2,1,0:T(8,128)S(1)} collective-permute-done((f32[4,1,8,128]{3,2,1,0:T(8,128)S(1)}, f32[4,1,8,128]{3,2,1,0:T(8,128)S(1)}, u32[]{:S(2)}, u32[]{:S(2)}) %collective-permute-start.1) | collective-permute-done | bytes 16416 | tf_op jit(solution)/shard_map/ppermute | solution.py:21
  61.4 6.1 %collective-permute-done = f32[4,1,8,128]{3,2,1,0:T(8,128)S(1)} collective-permute-done((f32[4,1,8,128]{3,2,1,0:T(8,128)S(1)}, f32[4,1,8,128]{3,2,1,0:T(8,128)S(1)}, u32[]{:S(2)}, u32[]{:S(2)}) %collective-permute-start) | collective-permute-done | bytes 16416 | tf_op jit(solution)/shard_map/ppermute | solution.py:22
  67.5 0.0 copy-start.2
  67.5 0.3 select_maximum_fusion
  67.8 0.4 copy-done.2
  68.2 0.1 fusion.4.diffused
  68.3 5.5 %all-to-all-done = f32[16,56,128]{2,1,0:T(8,128)S(1)} async-done(((f32[16,56,128]{2,1,0:T(8,128)}), f32[16,56,128]{2,1,0:T(8,128)S(1)}, u32[]{:S(2)}, u32[]{:S(2)}) %all-to-all-start) | async-done | bytes 458784 | tf_op jit(solution)/shard_map/all_to_all | solution.py:215
  73.7 7.5 %cells.1 = (f32[8,32,128]{2,1,0:T(8,128)S(1)}, f32[384,128]{1,0:T(8,128)}) custom-call(f32[896,128]{1,0:T(8,128)S(1)} %bitcast.8, f32[4,32,128]{2,1,0:T(8,128)S(1)} %fusion.4.diffused), custom_call_target="tpu_custom_call" | custom-call | tf_op jit(solution)/shard_map/cells/pallas_call | solution.py:217
  81.2 10.9 %all-to-all-start.1 = ((f32[16,24,128]{2,1,0:T(8,128)}), f32[16,24,128]{2,1,0:T(8,128)S(1)}, u32[]{:S(2)}, u32[]{:S(2)}) async-start(f32[16,24,128]{2,1,0:T(8,128)} %bitcast.5), calls=%async_computation.1 | async-start | bytes 393216 | tf_op jit(solution)/shard_map/all_to_all | solution.py:232
  92.2 0.0 copy-start
  92.2 0.6 divide_bitcast_fusion
  92.8 13.1 %all-to-all-done.1.came = f32[16,24,128]{2,1,0:T(8,128)S(1)} async-done(((f32[16,24,128]{2,1,0:T(8,128)}), f32[16,24,128]{2,1,0:T(8,128)S(1)}, u32[]{:S(2)}, u32[]{:S(2)}) %all-to-all-start.1) | async-done | bytes 196640 | tf_op jit(solution)/shard_map/all_to_all | solution.py:232
  105.9 0.0 copy-done
  105.9 1.3 %place.1 = f32[4,4096]{1,0:T(4,128)} custom-call(s32[32]{0:T(128)S(1)} %bitcast.10, f32[16,24,128]{2,1,0:T(8,128)S(1)} %all-to-all-done.1.came), custom_call_target="tpu_custom_call" | custom-call | tf_op jit(solution)/shard_map/place/pallas_call | solution.py:233
  (7 shorter events, 0.0 us)
Async XLA Ops:
  2.5 43.8 %copy-start.1 = (f32[4,4,8,128]{3,2,1,0:T(8,128)S(1)}, f32[4,4,8,128]{3,2,1,0:T(8,128)}, u32[]{:S(2)}) copy-start(f32[4,4,8,128]{3,2,1,0:T(8,128)} %param.6) | copy-start | bytes 196612
  2.5 71.2 %all-to-all-start = ((f32[16,56,128]{2,1,0:T(8,128)}), f32[16,56,128]{2,1,0:T(8,128)S(1)}, u32[]{:S(2)}, u32[]{:S(2)}) async-start(f32[16,56,128]{2,1,0:T(8,128)} %pack.1), calls=%async_computation | async-start | bytes 917504 | tf_op jit(solution)/shard_map/all_to_all | solution.py:215
  46.3 15.1 %collective-permute-start.1 = (f32[4,1,8,128]{3,2,1,0:T(8,128)S(1)}, f32[4,1,8,128]{3,2,1,0:T(8,128)S(1)}, u32[]{:S(2)}, u32[]{:S(2)}) collective-permute-start(f32[4,1,8,128]{3,2,1,0:T(8,128)S(1)} %get-tuple-element.9), channel_id=1, source_target_pairs={{0,16},{16,32},{32,48},{48,64},{64,80},{80,96},{96,112},{112,128},... | collective-permute-start | bytes 49160 | tf_op jit(solution)/shard_map/ppermute | solution.py:21
  50.0 6.2 %collective-permute-start.3 = (f32[4,4,1,128]{3,2,1,0:T(1,128)S(1)}, f32[4,4,1,128]{3,2,1,0:T(1,128)S(1)}, u32[]{:S(2)}, u32[]{:S(2)}) collective-permute-start(f32[4,4,1,128]{3,2,1,0:T(1,128)S(1)} %get-tuple-element.6), channel_id=1, source_target_pairs={{0,2},{2,4},{4,6},{6,8},{8,10},{10,12},{12,14},{1,3},{3,5},{5,7},{... | collective-permute-start | bytes 24584 | tf_op jit(solution)/shard_map/ppermute | solution.py:21
  53.6 5.6 %collective-permute-start.2 = (f32[4,4,1,128]{3,2,1,0:T(1,128)S(1)}, f32[4,4,1,128]{3,2,1,0:T(1,128)S(1)}, u32[]{:S(2)}, u32[]{:S(2)}) collective-permute-start(f32[4,4,1,128]{3,2,1,0:T(1,128)S(1)} %get-tuple-element.7), channel_id=1, source_target_pairs={{2,0},{4,2},{6,4},{8,6},{10,8},{12,10},{14,12},{3,1},{5,3},{7,5},{... | collective-permute-start | bytes 24584 | tf_op jit(solution)/shard_map/ppermute | solution.py:22
  54.9 12.6 %collective-permute-start = (f32[4,1,8,128]{3,2,1,0:T(8,128)S(1)}, f32[4,1,8,128]{3,2,1,0:T(8,128)S(1)}, u32[]{:S(2)}, u32[]{:S(2)}) collective-permute-start(f32[4,1,8,128]{3,2,1,0:T(8,128)S(1)} %get-tuple-element.8), channel_id=1, source_target_pairs={{16,0},{32,16},{48,32},{64,48},{80,64},{96,80},{112,96},{128,112},... | collective-permute-start | bytes 49160 | tf_op jit(solution)/shard_map/ppermute | solution.py:22
  67.5 0.7 copy-start.2
  81.2 24.7 %all-to-all-start.1 = ((f32[16,24,128]{2,1,0:T(8,128)}), f32[16,24,128]{2,1,0:T(8,128)S(1)}, u32[]{:S(2)}, u32[]{:S(2)}) async-start(f32[16,24,128]{2,1,0:T(8,128)} %bitcast.5), calls=%async_computation.1 | async-start | bytes 393216 | tf_op jit(solution)/shard_map/all_to_all | solution.py:232
  92.2 13.8 %copy-start = (s32[32,1]{0,1:T(1,128)S(1)}, s32[32,1]{0,1:T(1,128)}, u32[]{:S(2)}) copy-start(s32[32,1]{0,1:T(1,128)} %param.11) | copy-start | bytes 388

commit v3 on v2

--- a/solution.py
+++ b/solution.py
@@ -87,7 +87,7 @@
     return high, (x - high.astype(jnp.float32)).astype(jnp.bfloat16)
 
 
-GROUP = 4
+GROUP, PART = 32, 2
 BITS = 10
 
 
@@ -113,23 +113,22 @@
     return total
 
 
-def group_of(got, work, ids, g, highs, lanes):
-    codes = [work[g * GROUP + k] for k in range(GROUP)]
+def part_of(got, codes, ids, highs, lanes):
     mask = (1 << BITS) - 1
     v = [got[pl.ds((c >> BITS) & mask, 1), :].astype(jnp.int32) for c in codes]
     v = jnp.concatenate(v, axis=1)
     row = v // lanes
     high = jnp.where(v < 0, -1, row % highs)
     low = v % lanes + lanes * (row // highs)
-    many = GROUP * lanes
+    many = len(codes) * lanes
     here = lax.broadcasted_iota(jnp.int32, (highs, many), 0) == high
     lows = jnp.broadcast_to(low.astype(jnp.float32), (16, many)).astype(jnp.bfloat16)
     one, zero = jnp.bfloat16(1.0), jnp.bfloat16(0.0)
     tiles = []
     for t in range(2 * lanes // 16):
-        own = jnp.concatenate([ids[t * 16 : t * 16 + 16, :]] * GROUP, axis=1)
+        own = jnp.concatenate([ids[t * 16 : t * 16 + 16, :]] * len(codes), axis=1)
         tiles.append(jnp.where(own == lows, one, zero))
-    return codes, here, jnp.concatenate(tiles, axis=0)
+    return here, jnp.concatenate(tiles, axis=0)
 
 
 def cell_kernel(got, diffused, sums_out, back, acc, table, ids, work, *, slabs, subs):
@@ -143,16 +142,24 @@
     acc[...] = jnp.zeros(acc.shape, jnp.float32)
     ids[...] = lax.broadcasted_iota(jnp.int32, ids.shape, 0).astype(jnp.float32).astype(jnp.bfloat16)
 
+    def parts(g):
+        return [[work[g * GROUP + p + k] for k in range(PART)] for p in range(0, GROUP, PART)]
+
     def add(g, unused):
-        codes, here, onehot = group_of(got, work, ids, g, highs, lanes)
-        own = [got[pl.ds(pl.multiple_of(c & mask, 8), channels), :] for c in codes]
-        high, low = halves(jnp.concatenate(own, axis=1))
-        values = jnp.concatenate([high.astype(jnp.float32), low.astype(jnp.float32)], axis=0)
-        spread = jnp.where(here[None], values[:, None, :], 0.0).astype(jnp.bfloat16)
-        spread = spread.reshape(2 * channels * highs, GROUP * lanes)
-        acc[...] += lax.dot_general(
-            spread, onehot, (((1,), (1,)), ((), ())), preferred_element_type=jnp.float32
-        )
+        partial = []
+        for codes in parts(g):
+            here, onehot = part_of(got, codes, ids, highs, lanes)
+            own = [got[pl.ds(pl.multiple_of(c & mask, 8), channels), :] for c in codes]
+            high, low = halves(jnp.concatenate(own, axis=1))
+            values = jnp.concatenate([high.astype(jnp.float32), low.astype(jnp.float32)], axis=0)
+            spread = jnp.where(here[None], values[:, None, :], 0.0).astype(jnp.bfloat16)
+            spread = spread.reshape(2 * channels * highs, PART * lanes)
+            partial.append(
+                lax.dot_general(
+                    spread, onehot, (((1,), (1,)), ((), ())), preferred_element_type=jnp.float32
+                )
+            )
+        acc[...] += sum(partial[1:], partial[0])
         return unused
 
     lax.fori_loop(0, steps, add, 0)
@@ -165,12 +172,13 @@
     table[...] = jnp.concatenate(halves(by_low), axis=0)
 
     def read(g, unused):
-        codes, here, onehot = group_of(got, work, ids, g, highs, lanes)
-        rows = jnp.dot(table[...], onehot, preferred_element_type=jnp.float32)
-        rows = (rows[: subs * highs] + rows[subs * highs :]).reshape(subs, highs, GROUP * lanes)
-        found = jnp.sum(jnp.where(here[None], rows, 0.0), axis=1)
-        for k, c in enumerate(codes):
-            back[pl.ds(c >> 2 * BITS, subs), :] = found[:, k * lanes : (k + 1) * lanes]
+        for codes in parts(g):
+            here, onehot = part_of(got, codes, ids, highs, lanes)
+            rows = jnp.dot(table[...], onehot, preferred_element_type=jnp.float32)
+            rows = (rows[: subs * highs] + rows[subs * highs :]).reshape(subs, highs, PART * lanes)
+            found = jnp.sum(jnp.where(here[None], rows, 0.0), axis=1)
+            for k, c in enumerate(codes):
+                back[pl.ds(c >> 2 * BITS, subs), :] = found[:, k * lanes : (k + 1) * lanes]
         return unused
 
     lax.fori_loop(0, steps, read, 0)
@@ -186,6 +194,25 @@
 
 def smem():
     return pl.BlockSpec(memory_space=pltpu.SMEM)
+
+
+def call_cells(got, diffused, slabs, subs):
+    lines, lanes = diffused.shape[1:]
+    f32 = functools.partial(jax.ShapeDtypeStruct, dtype=jnp.float32)
+    return pl.pallas_call(
+        functools.partial(cell_kernel, slabs=slabs, subs=subs),
+        out_shape=(f32((2 * subs, lines, lanes)), f32((slabs * CAP * subs, lanes))),
+        in_specs=[vmem(), vmem()],
+        out_specs=(vmem(), vmem()),
+        scratch_shapes=[
+            pltpu.VMEM((4 * subs * lines // 2, 2 * lanes), jnp.float32),
+            pltpu.VMEM((2 * subs * lines // 2, 2 * lanes), jnp.bfloat16),
+            pltpu.VMEM((2 * lanes, lanes), jnp.bfloat16),
+            pltpu.SMEM((slabs * CAP + GROUP,), jnp.int32),
+        ],
+        compiler_params=small(8),
+        name="cells",
+    )(got, diffused)
 
 
 def shards(field, diffusion, secrete, uptake, cell_voxel, block_dest):
@@ -214,20 +241,7 @@
     )(dest, secrete, uptake, cell_voxel.reshape(blocks, cells))
     got = lax.all_to_all(sent, "gz", split_axis=0, concat_axis=0, tiled=True)
     diffused = diffuse(field, diffusion).reshape(subs, lines, lanes)
-    sums, back = pl.pallas_call(
-        functools.partial(cell_kernel, slabs=slabs, subs=subs),
-        out_shape=(f32((2 * subs, lines, lanes)), f32((slabs * CAP * subs, cells))),
-        in_specs=[vmem(), vmem()],
-        out_specs=(vmem(), vmem()),
-        scratch_shapes=[
-            pltpu.VMEM((4 * subs * lines // 2, 2 * lanes), jnp.float32),
-            pltpu.VMEM((2 * subs * lines // 2, 2 * lanes), jnp.bfloat16),
-            pltpu.VMEM((2 * lanes, lanes), jnp.bfloat16),
-            pltpu.SMEM((slabs * CAP + GROUP,), jnp.int32),
-        ],
-        compiler_params=small(8),
-        name="cells",
-    )(got.reshape(slabs * rows, cells), diffused)
+    sums, back = call_cells(got.reshape(slabs * rows, cells), diffused, slabs, subs)
     back = back.reshape(slabs, CAP * subs, cells)
     came = lax.all_to_all(back, "gz", split_axis=0, concat_axis=0, tiled=True)
     cell_conc = pl.pallas_call(

time: 108 us -> 103 us (0.954)
  Pallas kernels: 10.7 us -> 5.71 us
  starting transfers between devices: 64.6 us -> 61.6 us
  waiting for transfers between devices: 29.8 us -> 32.2 us
    pallas_call x1, Pallas kernels: 7.52 us -> 2.56 us  [call_cells(): pl.pallas_call(functools.partial(cell_kernel, slabs=slabs, subs=subs), ou...]
    all_to_all x1, starting transfers between devices: 10.9 us -> 7.9 us  [shards(): came = lax.all_to_all(back, 'gz', split_axis=0, concat_axis=0, tiled=True)]
    all_to_all x1, waiting for transfers between devices: 13.1 us -> 15.5 us  [shards(): came = lax.all_to_all(back, 'gz', split_axis=0, concat_axis=0, tiled=True)]
where the time goes in v3:
time: 103 us; the launch traced here: 102 us
  starting transfers between devices  61.6 us (60%)
  waiting for transfers between devices  32.2 us (31%)
  Pallas kernels  5.71 us (6%)
    all_to_all x1, starting transfers between devices, shards(): got = lax.all_to_all(sent, 'gz', split_axis=0, concat_axis=0, tiled=True)  43.8 us
    all_to_all x1, waiting for transfers between devices, shards(): came = lax.all_to_all(back, 'gz', split_axis=0, concat_axis=0, tiled=True)  15.5 us
    ppermute x2, waiting for transfers between devices, extended(): lax.ppermute(leading, axis, [(b, a) for a, b in up])  8.99 us
    all_to_all x1, starting transfers between devices, shards(): came = lax.all_to_all(back, 'gz', split_axis=0, concat_axis=0, tiled=True)  7.9 us
    ppermute x2, starting transfers between devices, extended(): lax.ppermute(last, axis, up)  7.21 us
    all_to_all x1, waiting for transfers between devices, shards(): got = lax.all_to_all(sent, 'gz', split_axis=0, concat_axis=0, tiled=True)  5.45 us
    ppermute x2, starting transfers between devices, extended(): lax.ppermute(leading, axis, [(b, a) for a, b in up])  2.62 us
    pallas_call x1, Pallas kernels, call_cells(): pl.pallas_call(functools.partial(cell_kernel, slabs=slabs, subs=subs), ou...  2.56 us
  transfers between devices with their start and end apart: 6, of which 5 were waited for; matrix products, arithmetic and copies ran while one was open for 1% of the time, Pallas kernels for 0%

profile of v3, /device:TPU:80, one launch (start us, length us, event | category | flops | bytes accessed | tf_op | source)
XLA Modules:
  0.0 101.7 jit_solution(14848971197897488481)
XLA Ops:
  0.6 1.8 %pack.1 = f32[16,56,128]{2,1,0:T(8,128)} custom-call(s32[32]{0:T(128)} %bitcast.9, f32[4,4096]{1,0:T(4,128)} %secrete_in.1, f32[4,4096]{1,0:T(4,128)} %uptake_in.1, s32[32,128]{1,0:T(8,128)} %bitcast.11), custom_call_target="tpu_custom_call" | custom-call | tf_op jit(solution)/shard_map/pack/pallas_call | solution.py:227
  2.5 0.0 copy-start.1
  2.5 43.8 %all-to-all-start = ((f32[16,56,128]{2,1,0:T(8,128)}), f32[16,56,128]{2,1,0:T(8,128)S(1)}, u32[]{:S(2)}, u32[]{:S(2)}) async-start(f32[16,56,128]{2,1,0:T(8,128)} %pack.1), calls=%async_computation | async-start | bytes 917504 | tf_op jit(solution)/shard_map/all_to_all | solution.py:242
  46.3 0.0 copy-done.1
  46.3 3.7 %collective-permute-start.1 = (f32[4,1,8,128]{3,2,1,0:T(8,128)S(1)}, f32[4,1,8,128]{3,2,1,0:T(8,128)S(1)}, u32[]{:S(2)}, u32[]{:S(2)}) collective-permute-start(f32[4,1,8,128]{3,2,1,0:T(8,128)S(1)} %get-tuple-element.9), channel_id=1, source_target_pairs={{0,16},{16,32},{32,48},{48,64},{64,80},{80,96},{96,112},{112,128},... | collective-permute-start | bytes 49160 | tf_op jit(solution)/shard_map/ppermute | solution.py:21
  50.0 3.6 %collective-permute-start.3 = (f32[4,4,1,128]{3,2,1,0:T(1,128)S(1)}, f32[4,4,1,128]{3,2,1,0:T(1,128)S(1)}, u32[]{:S(2)}, u32[]{:S(2)}) collective-permute-start(f32[4,4,1,128]{3,2,1,0:T(1,128)S(1)} %get-tuple-element.6), channel_id=1, source_target_pairs={{0,2},{2,4},{4,6},{6,8},{8,10},{10,12},{12,14},{1,3},{3,5},{5,7},{... | collective-permute-start | bytes 24584 | tf_op jit(solution)/shard_map/ppermute | solution.py:21
  53.6 1.3 %collective-permute-start.2 = (f32[4,4,1,128]{3,2,1,0:T(1,128)S(1)}, f32[4,4,1,128]{3,2,1,0:T(1,128)S(1)}, u32[]{:S(2)}, u32[]{:S(2)}) collective-permute-start(f32[4,4,1,128]{3,2,1,0:T(1,128)S(1)} %get-tuple-element.7), channel_id=1, source_target_pairs={{2,0},{4,2},{6,4},{8,6},{10,8},{12,10},{14,12},{3,1},{5,3},{7,5},{... | collective-permute-start | bytes 24584 | tf_op jit(solution)/shard_map/ppermute | solution.py:22
  54.9 1.3 %collective-permute-start = (f32[4,1,8,128]{3,2,1,0:T(8,128)S(1)}, f32[4,1,8,128]{3,2,1,0:T(8,128)S(1)}, u32[]{:S(2)}, u32[]{:S(2)}) collective-permute-start(f32[4,1,8,128]{3,2,1,0:T(8,128)S(1)} %get-tuple-element.8), channel_id=1, source_target_pairs={{16,0},{32,16},{48,32},{64,48},{80,64},{96,80},{112,96},{128,112},... | collective-permute-start | bytes 49160 | tf_op jit(solution)/shard_map/ppermute | solution.py:22
  56.2 0.0 collective-permute-done.3
  56.3 2.9 %collective-permute-done.2 = f32[4,4,1,128]{3,2,1,0:T(1,128)S(1)} collective-permute-done((f32[4,4,1,128]{3,2,1,0:T(1,128)S(1)}, f32[4,4,1,128]{3,2,1,0:T(1,128)S(1)}, u32[]{:S(2)}, u32[]{:S(2)}) %collective-permute-start.2) | collective-permute-done | bytes 8224 | tf_op jit(solution)/shard_map/ppermute | solution.py:22
  59.2 2.2 %collective-permute-done.1 = f32[4,1,8,128]{3,2,1,0:T(8,128)S(1)} collective-permute-done((f32[4,1,8,128]{3,2,1,0:T(8,128)S(1)}, f32[4,1,8,128]{3,2,1,0:T(8,128)S(1)}, u32[]{:S(2)}, u32[]{:S(2)}) %collective-permute-start.1) | collective-permute-done | bytes 16416 | tf_op jit(solution)/shard_map/ppermute | solution.py:21
  61.4 6.1 %collective-permute-done = f32[4,1,8,128]{3,2,1,0:T(8,128)S(1)} collective-permute-done((f32[4,1,8,128]{3,2,1,0:T(8,128)S(1)}, f32[4,1,8,128]{3,2,1,0:T(8,128)S(1)}, u32[]{:S(2)}, u32[]{:S(2)}) %collective-permute-start) | collective-permute-done | bytes 16416 | tf_op jit(solution)/shard_map/ppermute | solution.py:22
  67.5 0.0 copy-start.2
  67.5 0.3 select_maximum_fusion
  67.8 0.4 copy-done.2
  68.2 0.1 fusion.4.diffused
  68.3 5.5 %all-to-all-done = f32[16,56,128]{2,1,0:T(8,128)S(1)} async-done(((f32[16,56,128]{2,1,0:T(8,128)}), f32[16,56,128]{2,1,0:T(8,128)S(1)}, u32[]{:S(2)}, u32[]{:S(2)}) %all-to-all-start) | async-done | bytes 458784 | tf_op jit(solution)/shard_map/all_to_all | solution.py:242
  73.7 2.6 %cells.1 = (f32[8,32,128]{2,1,0:T(8,128)S(1)}, f32[384,128]{1,0:T(8,128)}) custom-call(f32[896,128]{1,0:T(8,128)S(1)} %bitcast.8, f32[4,32,128]{2,1,0:T(8,128)S(1)} %fusion.4.diffused), custom_call_target="tpu_custom_call" | custom-call | tf_op jit(solution)/shard_map/cells/pallas_call | solution.py:202
  76.3 7.9 %all-to-all-start.1 = ((f32[16,24,128]{2,1,0:T(8,128)}), f32[16,24,128]{2,1,0:T(8,128)S(1)}, u32[]{:S(2)}, u32[]{:S(2)}) async-start(f32[16,24,128]{2,1,0:T(8,128)} %bitcast.5), calls=%async_computation.1 | async-start | bytes 393216 | tf_op jit(solution)/shard_map/all_to_all | solution.py:246
  84.2 0.0 copy-start
  84.2 0.6 divide_bitcast_fusion
  84.8 15.5 %all-to-all-done.1.came = f32[16,24,128]{2,1,0:T(8,128)S(1)} async-done(((f32[16,24,128]{2,1,0:T(8,128)}), f32[16,24,128]{2,1,0:T(8,128)S(1)}, u32[]{:S(2)}, u32[]{:S(2)}) %all-to-all-start.1) | async-done | bytes 196640 | tf_op jit(solution)/shard_map/all_to_all | solution.py:246
  100.4 0.0 copy-done
  100.4 1.3 %place.1 = f32[4,4096]{1,0:T(4,128)} custom-call(s32[32]{0:T(128)S(1)} %bitcast.10, f32[16,24,128]{2,1,0:T(8,128)S(1)} %all-to-all-done.1.came), custom_call_target="tpu_custom_call" | custom-call | tf_op jit(solution)/shard_map/place/pallas_call | solution.py:247
  (7 shorter events, 0.0 us)
Async XLA Ops:
  2.5 43.8 %copy-start.1 = (f32[4,4,8,128]{3,2,1,0:T(8,128)S(1)}, f32[4,4,8,128]{3,2,1,0:T(8,128)}, u32[]{:S(2)}) copy-start(f32[4,4,8,128]{3,2,1,0:T(8,128)} %param.6) | copy-start | bytes 196612
  2.5 71.2 %all-to-all-start = ((f32[16,56,128]{2,1,0:T(8,128)}), f32[16,56,128]{2,1,0:T(8,128)S(1)}, u32[]{:S(2)}, u32[]{:S(2)}) async-start(f32[16,56,128]{2,1,0:T(8,128)} %pack.1), calls=%async_computation | async-start | bytes 917504 | tf_op jit(solution)/shard_map/all_to_all | solution.py:242
  46.3 15.1 %collective-permute-start.1 = (f32[4,1,8,128]{3,2,1,0:T(8,128)S(1)}, f32[4,1,8,128]{3,2,1,0:T(8,128)S(1)}, u32[]{:S(2)}, u32[]{:S(2)}) collective-permute-start(f32[4,1,8,128]{3,2,1,0:T(8,128)S(1)} %get-tuple-element.9), channel_id=1, source_target_pairs={{0,16},{16,32},{32,48},{48,64},{64,80},{80,96},{96,112},{112,128},... | collective-permute-start | bytes 49160 | tf_op jit(solution)/shard_map/ppermute | solution.py:21
  50.0 6.2 %collective-permute-start.3 = (f32[4,4,1,128]{3,2,1,0:T(1,128)S(1)}, f32[4,4,1,128]{3,2,1,0:T(1,128)S(1)}, u32[]{:S(2)}, u32[]{:S(2)}) collective-permute-start(f32[4,4,1,128]{3,2,1,0:T(1,128)S(1)} %get-tuple-element.6), channel_id=1, source_target_pairs={{0,2},{2,4},{4,6},{6,8},{8,10},{10,12},{12,14},{1,3},{3,5},{5,7},{... | collective-permute-start | bytes 24584 | tf_op jit(solution)/shard_map/ppermute | solution.py:21
  53.6 5.6 %collective-permute-start.2 = (f32[4,4,1,128]{3,2,1,0:T(1,128)S(1)}, f32[4,4,1,128]{3,2,1,0:T(1,128)S(1)}, u32[]{:S(2)}, u32[]{:S(2)}) collective-permute-start(f32[4,4,1,128]{3,2,1,0:T(1,128)S(1)} %get-tuple-element.7), channel_id=1, source_target_pairs={{2,0},{4,2},{6,4},{8,6},{10,8},{12,10},{14,12},{3,1},{5,3},{7,5},{... | collective-permute-start | bytes 24584 | tf_op jit(solution)/shard_map/ppermute | solution.py:22
  54.9 12.6 %collective-permute-start = (f32[4,1,8,128]{3,2,1,0:T(8,128)S(1)}, f32[4,1,8,128]{3,2,1,0:T(8,128)S(1)}, u32[]{:S(2)}, u32[]{:S(2)}) collective-permute-start(f32[4,1,8,128]{3,2,1,0:T(8,128)S(1)} %get-tuple-element.8), channel_id=1, source_target_pairs={{16,0},{32,16},{48,32},{64,48},{80,64},{96,80},{112,96},{128,112},... | collective-permute-start | bytes 49160 | tf_op jit(solution)/shard_map/ppermute | solution.py:22
  67.5 0.7 copy-start.2
  76.3 24.1 %all-to-all-start.1 = ((f32[16,24,128]{2,1,0:T(8,128)}), f32[16,24,128]{2,1,0:T(8,128)S(1)}, u32[]{:S(2)}, u32[]{:S(2)}) async-start(f32[16,24,128]{2,1,0:T(8,128)} %bitcast.5), calls=%async_computation.1 | async-start | bytes 393216 | tf_op jit(solution)/shard_map/all_to_all | solution.py:246
  84.2 16.2 %copy-start = (s32[32,1]{0,1:T(1,128)S(1)}, s32[32,1]{0,1:T(1,128)}, u32[]{:S(2)}) copy-start(s32[32,1]{0,1:T(1,128)} %param.11) | copy-start | bytes 388

commit v4 on v3

v4 whole, which is shorter than its diff:
```python
import functools

import jax
import jax.numpy as jnp
from jax import lax
from jax.experimental import pallas as pl
from jax.experimental.pallas import tpu as pltpu
from jax.sharding import PartitionSpec as P

CAP = 6


def extended(x, sides, width):
    edges = {}
    for axis, dim in sides:
        size, length = (lax.axis_size(axis), x.shape[dim])
        up = [(i, (i + 1) % size) for i in range(size - 1)]
        last = lax.slice_in_dim(x, length - width, length, axis=dim)
        leading = lax.slice_in_dim(x, 0, width, axis=dim)
        edges[dim] = (
            lax.ppermute(last, axis, up),
            lax.ppermute(leading, axis, [(b, a) for a, b in up]),
        )
    done = []
    for _, dim in sides:
        low, high = edges[dim]
        around = [(width, width) if d in done else (0, 0) for d in range(x.ndim)]
        x = jnp.concatenate([jnp.pad(low, around), x, jnp.pad(high, around)], axis=dim)
        done.append(dim)
    return x


def neighbours(padded):
    beside_all = padded[:, 2:, 1:-1, 1:-1] + padded[:, :-2, 1:-1, 1:-1]
    beside_all = beside_all + padded[:, 1:-1, 2:, 1:-1] + padded[:, 1:-1, :-2, 1:-1]
    return beside_all + padded[:, 1:-1, 1:-1, 2:] + padded[:, 1:-1, 1:-1, :-2]


def diffuse(field, diffusion):
    padded = extended(field, (("gz", 1), ("gy", 2)), 1)
    padded = jnp.pad(padded, ((0, 0), (0, 0), (0, 0), (1, 1)))
    return field + diffusion[:, None, None, None] * (neighbours(padded) - 6.0 * field)


def rows_of(channels):
    return CAP * channels, CAP * channels + CAP


def pack_kernel(
    dest_in, secrete_in, uptake_in, voxel_in, out, dest, secrete, uptake, voxel, used, sems, *, slabs, subs
):
    pairs = ((dest_in, dest), (secrete_in, secrete), (uptake_in, uptake), (voxel_in, voxel))
    copies = [pltpu.make_async_copy(a, b, sems.at[i]) for i, (a, b) in enumerate(pairs)]
    for copy in copies:
        copy.start()
    cells = out.shape[1]
    base, rows = rows_of(2 * subs)
    for i in range(slabs):
        out[i * rows + base : (i + 1) * rows, :] = jnp.full((rows - base, cells), -1.0, jnp.float32)
        used[i] = 0
    for copy in copies:
        copy.wait()
    for b in range(dest.shape[0]):
        to = dest[b]
        slot = used[to]
        used[to] = slot + 1
        at = slice(b * cells, (b + 1) * cells)
        first = to * rows + slot * 2 * subs
        out[pl.ds(first, subs), :] = secrete[:, at]
        out[pl.ds(first + subs, subs), :] = uptake[:, at]
        out[pl.ds(to * rows + base + slot, 1), :] = voxel[b : b + 1, :].astype(jnp.float32)


def place_kernel(dest, came, out, used, *, blocks, cells, subs):
    for i in range(came.shape[0]):
        used[i] = 0
    for b in range(blocks):
        to = dest[b]
        slot = used[to]
        used[to] = slot + 1
        out[:, b * cells : (b + 1) * cells] = came[to, pl.ds(slot * subs, subs), :]


def halves(x):
    high = x.astype(jnp.bfloat16)
    return high, (x - high.astype(jnp.float32)).astype(jnp.bfloat16)


GROUP, PART = 48, 2
BITS = 10


def list_blocks(got, work, high_of, low_of, slabs, subs, highs):
    base, rows = rows_of(2 * subs)
    lanes = got.shape[1]
    lane_bits, high_bits = lanes.bit_length() - 1, highs.bit_length() - 1
    lane = lax.broadcasted_iota(jnp.int32, (CAP, lanes), 1)
    words, total, hole = [], jnp.int32(0), jnp.int32(0)
    for w in range(slabs // 8):
        marks = jnp.zeros((CAP, lanes), jnp.float32)
        for k in range(8):
            i = w * 8 + k
            v = got[i * rows + base : (i + 1) * rows, :].astype(jnp.int32)
            row = v >> lane_bits
            here = v >= 0
            high = jnp.where(here, row & (highs - 1), -1)
            low = (v & (lanes - 1)) | ((row >> high_bits) << lane_bits)
            high_of[i * CAP : (i + 1) * CAP, :] = high.astype(jnp.float32)
            low_of[i * CAP : (i + 1) * CAP, :] = low.astype(jnp.float32)
            marks = marks + jnp.where(here & (lane == 0), float(8**k), 0.0)
        words.append(jnp.sum(marks).astype(jnp.int32))
    for i in range(slabs):
        count = (words[i // 8] >> (3 * (i % 8))) & 7
        for slot in range(CAP):
            at = i * rows + slot * 2 * subs, i * CAP + slot, (i * CAP + slot) * subs
            code = at[0] | at[1] << BITS | at[2] << 2 * BITS
            work[total + slot] = code
        hole = jnp.where(count < CAP, code, hole)
        total = total + count
    for k in range(GROUP - 1):
        work[total + k] = hole
    return total


def spread_row(ref, row):
    own = ref[pl.ds(row, 8, stride=0), :]
    return jnp.concatenate([own, own], axis=0).astype(jnp.bfloat16)


def onehots_of(ids, lows, wide):
    tiles = []
    for t in range(0, wide, 16):
        own = ids[t : t + 16, :].astype(jnp.bfloat16)
        row = [jnp.where(own == low, jnp.bfloat16(1.0), jnp.bfloat16(0.0)) for low in lows]
        tiles.append(jnp.concatenate(row, axis=1))
    return jnp.concatenate(tiles, axis=0)


def cell_kernel(
    got, diffused, sums_out, back, acc, table, ids, high_of, low_of, split, found, work, *, slabs, subs
):
    lanes = got.shape[1]
    channels = 2 * subs
    highs = diffused.shape[1] // 2
    wide = 2 * lanes
    mask = (1 << BITS) - 1
    total = list_blocks(got, work, high_of, low_of, slabs, subs, highs)
    steps = (total + GROUP - 1) // GROUP
    acc[...] = jnp.zeros(acc.shape, jnp.float32)
    ids[...] = lax.broadcasted_iota(jnp.int32, ids.shape, 0).astype(jnp.float32)

    def add(g, unused):
        partial = []
        first = ids[0:highs, :].astype(jnp.bfloat16)
        for p in range(0, GROUP, PART):
            spreads, lows = [], []
            for k in range(p, p + PART):
                code = work[g * GROUP + k]
                slot = (code >> BITS) & mask
                high, low = halves(got[pl.ds(code & mask, channels), :])
                at = k * 2 * channels
                split[at : at + channels, :] = high.astype(jnp.float32)
                split[at + channels : at + 2 * channels, :] = low.astype(jnp.float32)
                here = first == spread_row(high_of, slot)
                own = [jnp.where(here, spread_row(split, at + r), jnp.bfloat16(0.0)) for r in range(2 * channels)]
                spreads.append(jnp.concatenate(own, axis=0))
                lows.append(spread_row(low_of, slot))
            partial.append(
                lax.dot_general(
                    jnp.concatenate(spreads, axis=1),
                    onehots_of(ids, lows, wide),
                    (((1,), (1,)), ((), ())),
                    preferred_element_type=jnp.float32,
                )
            )
        acc[...] += sum(partial[1:], partial[0])
        return unused

    lax.fori_loop(0, steps, add, 0)
    half = channels * highs
    sums = (acc[0:half, :] + acc[half : 2 * half, :]).reshape(channels, highs, wide)
    sums = jnp.concatenate([sums[:, :, :lanes], sums[:, :, lanes:]], axis=1)
    sums_out[...] = sums
    new = (diffused[...] + sums[:subs]) / (1.0 + sums[subs:])
    by_low = jnp.concatenate([new[:, :highs], new[:, highs:]], axis=2).reshape(subs * highs, wide)
    table[...] = jnp.concatenate([h.astype(jnp.float32) for h in halves(by_low)], axis=0)

    sub = lax.broadcasted_iota(jnp.int32, (8, lanes), 0)
    subf = sub.astype(jnp.float32)

    def read(g, unused):
        values = table[...].astype(jnp.bfloat16)
        for p in range(0, GROUP, PART):
            codes = [work[g * GROUP + k] for k in range(p, p + PART)]
            slots = [(code >> BITS) & mask for code in codes]
            onehot = onehots_of(ids, [spread_row(low_of, slot) for slot in slots], wide)
            rows = jnp.dot(values, onehot, preferred_element_type=jnp.float32)
            rows = rows[: subs * highs] + rows[subs * highs :]
            for k in range(PART):
                own = rows[:, k * lanes : (k + 1) * lanes]
                high = high_of[pl.ds(slots[k], 8, stride=0), :]
                at = 8 * (p + k)
                found[at : at + 8, :] = found_rows(own, subf == high, subf + 8.0 == high, sub, subs, highs)
                back[pl.ds(codes[k] >> 2 * BITS, subs), :] = found[pl.ds(at + 1, subs, stride=2), :]
        return unused

    lax.fori_loop(0, steps, read, 0)


def found_rows(own, first, second, sub, subs, highs):
    assert subs == 4 and highs == 16
    fours = []
    for s in range(subs):
        a = own[s * highs : s * highs + 8, :]
        b = own[s * highs + 8 : s * highs + 16, :]
        x = jnp.where(first, a, jnp.where(second, b, 0.0))
        fours.append(x + pltpu.roll(x, 4, 0))
    upper = jnp.where(sub < 4, fours[1], fours[3])
    lower = jnp.where(sub < 4, fours[0], fours[2])
    upper = upper + pltpu.roll(upper, 2, 0)
    lower = lower + pltpu.roll(lower, 2, 0)
    both = jnp.where((sub & 2) == 2, upper, pltpu.roll(lower, 6, 0))
    return both + pltpu.roll(both, 1, 0)


def small(mebibytes):
    return pltpu.CompilerParams(vmem_limit_bytes=mebibytes << 20)


def vmem():
    return pl.BlockSpec(memory_space=pltpu.VMEM)


def smem():
    return pl.BlockSpec(memory_space=pltpu.SMEM)


def call_cells(got, diffused, slabs, subs):
    lines, lanes = diffused.shape[1:]
    f32 = functools.partial(jax.ShapeDtypeStruct, dtype=jnp.float32)
    return pl.pallas_call(
        functools.partial(cell_kernel, slabs=slabs, subs=subs),
        out_shape=(f32((2 * subs, lines, lanes)), f32((slabs * CAP * subs, lanes))),
        in_specs=[vmem(), vmem()],
        out_specs=(vmem(), vmem()),
        scratch_shapes=[
            pltpu.VMEM((4 * subs * lines // 2, 2 * lanes), jnp.float32),
            pltpu.VMEM((2 * subs * lines // 2, 2 * lanes), jnp.float32),
            pltpu.VMEM((2 * lanes, lanes), jnp.float32),
            pltpu.VMEM((slabs * CAP, lanes), jnp.float32),
            pltpu.VMEM((slabs * CAP, lanes), jnp.float32),
            pltpu.VMEM((GROUP * 4 * subs, lanes), jnp.float32),
            pltpu.VMEM((GROUP * 8, lanes), jnp.float32),
            pltpu.SMEM((slabs * CAP + GROUP + CAP,), jnp.int32),
        ],
        compiler_params=small(8),
        name="cells",
    )(got, diffused)


def shards(field, diffusion, secrete, uptake, cell_voxel, block_dest):
    subs, lanes = field.shape[0], field.shape[3]
    lines = field.shape[1] * field.shape[2]
    blocks = block_dest.shape[0]
    cells = secrete.shape[1] // blocks
    slabs = lax.axis_size("gz")
    base, rows = rows_of(2 * subs)
    f32 = functools.partial(jax.ShapeDtypeStruct, dtype=jnp.float32)
    dest = block_dest.reshape(blocks)
    sent = pl.pallas_call(
        functools.partial(pack_kernel, slabs=slabs, subs=subs),
        out_shape=f32((slabs * rows, cells)),
        in_specs=[pl.BlockSpec(memory_space=pltpu.HBM)] * 4,
        out_specs=vmem(),
        scratch_shapes=[
            pltpu.SMEM((blocks,), jnp.int32),
            pltpu.VMEM((subs, blocks * cells), jnp.float32),
            pltpu.VMEM((subs, blocks * cells), jnp.float32),
            pltpu.VMEM((blocks, cells), jnp.int32),
            pltpu.SMEM((slabs,), jnp.int32),
            pltpu.SemaphoreType.DMA((4,)),
        ],
        name="pack",
    )(dest, secrete, uptake, cell_voxel.reshape(blocks, cells))
    sent = sent.reshape(slabs, rows // 2, 2, cells)
    got = lax.all_to_all(sent, "gz", split_axis=0, concat_axis=0, tiled=True)
    diffused = diffuse(field, diffusion).reshape(subs, lines, lanes)
    sums, back = call_cells(got.reshape(slabs * rows, cells), diffused, slabs, subs)
    back = back.reshape(slabs, CAP * subs, cells)
    came = lax.all_to_all(back, "gz", split_axis=0, concat_axis=0, tiled=True)
    cell_conc = pl.pallas_call(
        functools.partial(place_kernel, blocks=blocks, cells=cells, subs=subs),
        out_shape=f32((subs, blocks * cells)),
        in_specs=[smem(), vmem()],
        out_specs=vmem(),
        scratch_shapes=[pltpu.SMEM((slabs,), jnp.int32)],
        compiler_params=small(4),
        name="place",
    )(dest, came)
    new_field = (diffused + sums[:subs]) / (1.0 + sums[subs:])
    return (new_field.reshape(field.shape), cell_conc)


def solution(mesh):
    in_specs = (
        P("sa", ("grp", "gz"), "gy", None),
        P("sa"),
        P("sa", ("grp", "gz", "gy")),
        P("sa", ("grp", "gz", "gy")),
        P(("grp", "gz", "gy")),
        P(("grp", "gz", "gy"), None),
    )
    out_specs = (P("sa", ("grp", "gz"), "gy", None), P("sa", ("grp", "gz", "gy")))
    return jax.shard_map(shards, mesh=mesh, in_specs=in_specs, out_specs=out_specs, check_vma=False)
```

time: 103 us -> 102 us (level)
  no operation moved by 1% of the time
where the time goes in v4:
time: 102 us; the launch traced here: 101 us
  starting transfers between devices  61.6 us (60%)
  waiting for transfers between devices  31.7 us (31%)
  Pallas kernels  5.77 us (6%)
    all_to_all x1, starting transfers between devices, shards(): got = lax.all_to_all(sent, 'gz', split_axis=0, concat_axis=0, tiled=True)  43.8 us
    all_to_all x1, waiting for transfers between devices, shards(): came = lax.all_to_all(back, 'gz', split_axis=0, concat_axis=0, tiled=True)  15.6 us
    ppermute x2, waiting for transfers between devices, extended(): lax.ppermute(leading, axis, [(b, a) for a, b in up])  8.97 us
    all_to_all x1, starting transfers between devices, shards(): came = lax.all_to_all(back, 'gz', split_axis=0, concat_axis=0, tiled=True)  7.9 us
    ppermute x2, starting transfers between devices, extended(): lax.ppermute(last, axis, up)  7.21 us
    all_to_all x1, waiting for transfers between devices, shards(): got = lax.all_to_all(sent, 'gz', split_axis=0, concat_axis=0, tiled=True)  5.63 us
    pallas_call x1, Pallas kernels, call_cells(): pl.pallas_call(functools.partial(cell_kernel, slabs=slabs, subs=subs), ou...  2.63 us
    ppermute x2, starting transfers between devices, extended(): lax.ppermute(leading, axis, [(b, a) for a, b in up])  2.62 us
  transfers between devices with their start and end apart: 6, of which 5 were waited for; matrix products, arithmetic and copies ran while one was open for 1% of the time, Pallas kernels for 0%

profile of v4, /device:TPU:80, one launch (start us, length us, event | category | flops | bytes accessed | tf_op | source)
XLA Modules:
  0.0 101.3 jit_solution(7076858001856114140)
XLA Ops:
  0.6 1.8 %pack.1 = f32[864,128]{1,0:T(8,128)} custom-call(s32[32]{0:T(128)} %bitcast.10, f32[4,4096]{1,0:T(4,128)} %secrete_in.1, f32[4,4096]{1,0:T(4,128)} %uptake_in.1, s32[32,128]{1,0:T(8,128)} %bitcast.13), custom_call_target="tpu_custom_call" | custom-call | tf_op jit(solution)/shard_map/pack/pallas_call | solution.py:270
  2.5 0.0 copy-start.1
  2.5 43.8 %all-to-all-start = ((f32[16,27,2,128]{3,2,1,0:T(2,128)}), f32[16,27,2,128]{3,2,1,0:T(2,128)S(1)}, u32[]{:S(2)}, u32[]{:S(2)}) async-start(f32[16,27,2,128]{3,2,1,0:T(2,128)} %bitcast.12), calls=%async_computation | async-start | bytes 884736 | tf_op jit(solution)/shard_map/all_to_all | solution.py:286
  46.3 0.0 copy-done.1
  46.3 3.7 %collective-permute-start.1 = (f32[4,1,8,128]{3,2,1,0:T(8,128)S(1)}, f32[4,1,8,128]{3,2,1,0:T(8,128)S(1)}, u32[]{:S(2)}, u32[]{:S(2)}) collective-permute-start(f32[4,1,8,128]{3,2,1,0:T(8,128)S(1)} %get-tuple-element.9), channel_id=1, source_target_pairs={{0,16},{16,32},{32,48},{48,64},{64,80},{80,96},{96,112},{112,128},... | collective-permute-start | bytes 49160 | tf_op jit(solution)/shard_map/ppermute | solution.py:21
  50.0 3.6 %collective-permute-start.3 = (f32[4,4,1,128]{3,2,1,0:T(1,128)S(1)}, f32[4,4,1,128]{3,2,1,0:T(1,128)S(1)}, u32[]{:S(2)}, u32[]{:S(2)}) collective-permute-start(f32[4,4,1,128]{3,2,1,0:T(1,128)S(1)} %get-tuple-element.6), channel_id=1, source_target_pairs={{0,2},{2,4},{4,6},{6,8},{8,10},{10,12},{12,14},{1,3},{3,5},{5,7},{... | collective-permute-start | bytes 24584 | tf_op jit(solution)/shard_map/ppermute | solution.py:21
  53.6 1.3 %collective-permute-start.2 = (f32[4,4,1,128]{3,2,1,0:T(1,128)S(1)}, f32[4,4,1,128]{3,2,1,0:T(1,128)S(1)}, u32[]{:S(2)}, u32[]{:S(2)}) collective-permute-start(f32[4,4,1,128]{3,2,1,0:T(1,128)S(1)} %get-tuple-element.7), channel_id=1, source_target_pairs={{2,0},{4,2},{6,4},{8,6},{10,8},{12,10},{14,12},{3,1},{5,3},{7,5},{... | collective-permute-start | bytes 24584 | tf_op jit(solution)/shard_map/ppermute | solution.py:22
  54.9 1.3 %collective-permute-start = (f32[4,1,8,128]{3,2,1,0:T(8,128)S(1)}, f32[4,1,8,128]{3,2,1,0:T(8,128)S(1)}, u32[]{:S(2)}, u32[]{:S(2)}) collective-permute-start(f32[4,1,8,128]{3,2,1,0:T(8,128)S(1)} %get-tuple-element.8), channel_id=1, source_target_pairs={{16,0},{32,16},{48,32},{64,48},{80,64},{96,80},{112,96},{128,112},... | collective-permute-start | bytes 49160 | tf_op jit(solution)/shard_map/ppermute | solution.py:22
  56.2 0.0 collective-permute-done.3
  56.2 2.9 %collective-permute-done.2 = f32[4,4,1,128]{3,2,1,0:T(1,128)S(1)} collective-permute-done((f32[4,4,1,128]{3,2,1,0:T(1,128)S(1)}, f32[4,4,1,128]{3,2,1,0:T(1,128)S(1)}, u32[]{:S(2)}, u32[]{:S(2)}) %collective-permute-start.2) | collective-permute-done | bytes 8224 | tf_op jit(solution)/shard_map/ppermute | solution.py:22
  59.2 1.5 %collective-permute-done.1 = f32[4,1,8,128]{3,2,1,0:T(8,128)S(1)} collective-permute-done((f32[4,1,8,128]{3,2,1,0:T(8,128)S(1)}, f32[4,1,8,128]{3,2,1,0:T(8,128)S(1)}, u32[]{:S(2)}, u32[]{:S(2)}) %collective-permute-start.1) | collective-permute-done | bytes 16416 | tf_op jit(solution)/shard_map/ppermute | solution.py:21
  60.7 6.1 %collective-permute-done = f32[4,1,8,128]{3,2,1,0:T(8,128)S(1)} collective-permute-done((f32[4,1,8,128]{3,2,1,0:T(8,128)S(1)}, f32[4,1,8,128]{3,2,1,0:T(8,128)S(1)}, u32[]{:S(2)}, u32[]{:S(2)}) %collective-permute-start) | collective-permute-done | bytes 16416 | tf_op jit(solution)/shard_map/ppermute | solution.py:22
  66.8 0.0 copy-start.2
  66.8 0.3 select_maximum_fusion
  67.1 0.4 copy-done.2
  67.5 0.1 fusion.4.diffused
  67.6 5.6 %all-to-all-done = f32[16,27,2,128]{3,2,1,0:T(2,128)S(1)} async-done(((f32[16,27,2,128]{3,2,1,0:T(2,128)}), f32[16,27,2,128]{3,2,1,0:T(2,128)S(1)}, u32[]{:S(2)}, u32[]{:S(2)}) %all-to-all-start) | async-done | bytes 442400 | tf_op jit(solution)/shard_map/all_to_all | solution.py:286
  73.2 2.6 %cells.1 = (f32[8,32,128]{2,1,0:T(8,128)S(1)}, f32[384,128]{1,0:T(8,128)}) custom-call(f32[864,128]{1,0:T(8,128)S(1)} %bitcast.9, f32[4,32,128]{2,1,0:T(8,128)S(1)} %fusion.4.diffused), custom_call_target="tpu_custom_call" | custom-call | tf_op jit(solution)/shard_map/cells/pallas_call | solution.py:241
  75.8 7.9 %all-to-all-start.1 = ((f32[16,24,128]{2,1,0:T(8,128)}), f32[16,24,128]{2,1,0:T(8,128)S(1)}, u32[]{:S(2)}, u32[]{:S(2)}) async-start(f32[16,24,128]{2,1,0:T(8,128)} %bitcast.6), calls=%async_computation.1 | async-start | bytes 393216 | tf_op jit(solution)/shard_map/all_to_all | solution.py:290
  83.7 0.0 copy-start
  83.7 0.6 divide_bitcast_fusion
  84.4 15.6 %all-to-all-done.1.came = f32[16,24,128]{2,1,0:T(8,128)S(1)} async-done(((f32[16,24,128]{2,1,0:T(8,128)}), f32[16,24,128]{2,1,0:T(8,128)S(1)}, u32[]{:S(2)}, u32[]{:S(2)}) %all-to-all-start.1) | async-done | bytes 196640 | tf_op jit(solution)/shard_map/all_to_all | solution.py:290
  99.9 0.0 copy-done
  99.9 1.3 %place.1 = f32[4,4096]{1,0:T(4,128)} custom-call(s32[32]{0:T(128)S(1)} %bitcast.11, f32[16,24,128]{2,1,0:T(8,128)S(1)} %all-to-all-done.1.came), custom_call_target="tpu_custom_call" | custom-call | tf_op jit(solution)/shard_map/place/pallas_call | solution.py:291
  (7 shorter events, 0.0 us)
Async XLA Ops:
  2.5 43.8 %copy-start.1 = (f32[4,4,8,128]{3,2,1,0:T(8,128)S(1)}, f32[4,4,8,128]{3,2,1,0:T(8,128)}, u32[]{:S(2)}) copy-start(f32[4,4,8,128]{3,2,1,0:T(8,128)} %param.6) | copy-start | bytes 196612
  2.5 70.7 %all-to-all-start = ((f32[16,27,2,128]{3,2,1,0:T(2,128)}), f32[16,27,2,128]{3,2,1,0:T(2,128)S(1)}, u32[]{:S(2)}, u32[]{:S(2)}) async-start(f32[16,27,2,128]{3,2,1,0:T(2,128)} %bitcast.12), calls=%async_computation | async-start | bytes 884736 | tf_op jit(solution)/shard_map/all_to_all | solution.py:286
  46.3 14.4 %collective-permute-start.1 = (f32[4,1,8,128]{3,2,1,0:T(8,128)S(1)}, f32[4,1,8,128]{3,2,1,0:T(8,128)S(1)}, u32[]{:S(2)}, u32[]{:S(2)}) collective-permute-start(f32[4,1,8,128]{3,2,1,0:T(8,128)S(1)} %get-tuple-element.9), channel_id=1, source_target_pairs={{0,16},{16,32},{32,48},{48,64},{64,80},{80,96},{96,112},{112,128},... | collective-permute-start | bytes 49160 | tf_op jit(solution)/shard_map/ppermute | solution.py:21
  50.0 6.2 %collective-permute-start.3 = (f32[4,4,1,128]{3,2,1,0:T(1,128)S(1)}, f32[4,4,1,128]{3,2,1,0:T(1,128)S(1)}, u32[]{:S(2)}, u32[]{:S(2)}) collective-permute-start(f32[4,4,1,128]{3,2,1,0:T(1,128)S(1)} %get-tuple-element.6), channel_id=1, source_target_pairs={{0,2},{2,4},{4,6},{6,8},{8,10},{10,12},{12,14},{1,3},{3,5},{5,7},{... | collective-permute-start | bytes 24584 | tf_op jit(solution)/shard_map/ppermute | solution.py:21
  53.6 5.6 %collective-permute-start.2 = (f32[4,4,1,128]{3,2,1,0:T(1,128)S(1)}, f32[4,4,1,128]{3,2,1,0:T(1,128)S(1)}, u32[]{:S(2)}, u32[]{:S(2)}) collective-permute-start(f32[4,4,1,128]{3,2,1,0:T(1,128)S(1)} %get-tuple-element.7), channel_id=1, source_target_pairs={{2,0},{4,2},{6,4},{8,6},{10,8},{12,10},{14,12},{3,1},{5,3},{7,5},{... | collective-permute-start | bytes 24584 | tf_op jit(solution)/shard_map/ppermute | solution.py:22
  54.9 11.9 %collective-permute-start = (f32[4,1,8,128]{3,2,1,0:T(8,128)S(1)}, f32[4,1,8,128]{3,2,1,0:T(8,128)S(1)}, u32[]{:S(2)}, u32[]{:S(2)}) collective-permute-start(f32[4,1,8,128]{3,2,1,0:T(8,128)S(1)} %get-tuple-element.8), channel_id=1, source_target_pairs={{16,0},{32,16},{48,32},{64,48},{80,64},{96,80},{112,96},{128,112},... | collective-permute-start | bytes 49160 | tf_op jit(solution)/shard_map/ppermute | solution.py:22
  66.8 0.7 copy-start.2
  75.8 24.1 %all-to-all-start.1 = ((f32[16,24,128]{2,1,0:T(8,128)}), f32[16,24,128]{2,1,0:T(8,128)S(1)}, u32[]{:S(2)}, u32[]{:S(2)}) async-start(f32[16,24,128]{2,1,0:T(8,128)} %bitcast.6), calls=%async_computation.1 | async-start | bytes 393216 | tf_op jit(solution)/shard_map/all_to_all | solution.py:290
  83.7 16.2 %copy-start = (s32[32,1]{0,1:T(1,128)S(1)}, s32[32,1]{0,1:T(1,128)}, u32[]{:S(2)}) copy-start(s32[32,1]{0,1:T(1,128)} %param.11) | copy-start | bytes 388

commit v5 on v4

--- a/solution.py
+++ b/solution.py
@@ -71,14 +71,15 @@
         out[pl.ds(to * rows + base + slot, 1), :] = voxel[b : b + 1, :].astype(jnp.float32)
 
 
-def place_kernel(dest, came, out, used, *, blocks, cells, subs):
-    for i in range(came.shape[0]):
-        used[i] = 0
+def place_kernel(first, came, new, out, new_field, used, *, blocks, cells, subs):
+    new_field[...] = new[...]
+    for i in range(0, came.shape[0] // subs, CAP):
+        used[i] = i
     for b in range(blocks):
-        to = dest[b]
-        slot = used[to]
-        used[to] = slot + 1
-        out[:, b * cells : (b + 1) * cells] = came[to, pl.ds(slot * subs, subs), :]
+        slab = first[b]
+        slot = used[slab]
+        used[slab] = slot + 1
+        out[:, b * cells : (b + 1) * cells] = came[pl.ds(slot * subs, subs), :]
 
 
 def halves(x):
@@ -86,7 +87,7 @@
     return high, (x - high.astype(jnp.float32)).astype(jnp.bfloat16)
 
 
-GROUP, PART = 48, 2
+SIZES, PART = (32, 40, 48, 96), 2
 BITS = 10
 
 
@@ -117,7 +118,7 @@
             work[total + slot] = code
         hole = jnp.where(count < CAP, code, hole)
         total = total + count
-    for k in range(GROUP - 1):
+    for k in range(SIZES[-1] // 2):
         work[total + k] = hole
     return total
 
@@ -137,7 +138,7 @@
 
 
 def cell_kernel(
-    got, diffused, sums_out, back, acc, table, ids, high_of, low_of, split, found, work, *, slabs, subs
+    got, diffused, dest_in, new_out, back, dest_out, acc, table, ids, high_of, low_of, split, found, work, *, slabs, subs
 ):
     lanes = got.shape[1]
     channels = 2 * subs
@@ -145,17 +146,21 @@
     wide = 2 * lanes
     mask = (1 << BITS) - 1
     total = list_blocks(got, work, high_of, low_of, slabs, subs, highs)
-    steps = (total + GROUP - 1) // GROUP
-    acc[...] = jnp.zeros(acc.shape, jnp.float32)
     ids[...] = lax.broadcasted_iota(jnp.int32, ids.shape, 0).astype(jnp.float32)
 
-    def add(g, unused):
+    def at_size(body):
+        below = -1
+        for size in SIZES:
+            pl.when((total > below) & (total <= size))(functools.partial(body, size))
+            below = size
+
+    def add(size):
         partial = []
         first = ids[0:highs, :].astype(jnp.bfloat16)
-        for p in range(0, GROUP, PART):
+        for p in range(0, size, PART):
             spreads, lows = [], []
             for k in range(p, p + PART):
-                code = work[g * GROUP + k]
+                code = work[k]
                 slot = (code >> BITS) & mask
                 high, low = halves(got[pl.ds(code & mask, channels), :])
                 at = k * 2 * channels
@@ -173,25 +178,25 @@
                     preferred_element_type=jnp.float32,
                 )
             )
-        acc[...] += sum(partial[1:], partial[0])
-        return unused
-
-    lax.fori_loop(0, steps, add, 0)
+        acc[...] = sum(partial[1:], partial[0])
+
+    at_size(add)
     half = channels * highs
     sums = (acc[0:half, :] + acc[half : 2 * half, :]).reshape(channels, highs, wide)
     sums = jnp.concatenate([sums[:, :, :lanes], sums[:, :, lanes:]], axis=1)
-    sums_out[...] = sums
     new = (diffused[...] + sums[:subs]) / (1.0 + sums[subs:])
+    new_out[...] = new
+    dest_out[...] = dest_in[...]
     by_low = jnp.concatenate([new[:, :highs], new[:, highs:]], axis=2).reshape(subs * highs, wide)
     table[...] = jnp.concatenate([h.astype(jnp.float32) for h in halves(by_low)], axis=0)
 
     sub = lax.broadcasted_iota(jnp.int32, (8, lanes), 0)
     subf = sub.astype(jnp.float32)
 
-    def read(g, unused):
+    def read(size):
         values = table[...].astype(jnp.bfloat16)
-        for p in range(0, GROUP, PART):
-            codes = [work[g * GROUP + k] for k in range(p, p + PART)]
+        for p in range(0, size, PART):
+            codes = [work[k] for k in range(p, p + PART)]
             slots = [(code >> BITS) & mask for code in codes]
             onehot = onehots_of(ids, [spread_row(low_of, slot) for slot in slots], wide)
             rows = jnp.dot(values, onehot, preferred_element_type=jnp.float32)
@@ -202,9 +207,8 @@
                 at = 8 * (p + k)
                 found[at : at + 8, :] = found_rows(own, subf == high, subf + 8.0 == high, sub, subs, highs)
                 back[pl.ds(codes[k] >> 2 * BITS, subs), :] = found[pl.ds(at + 1, subs, stride=2), :]
-        return unused
-
-    lax.fori_loop(0, steps, read, 0)
+
+    at_size(read)
 
 
 def found_rows(own, first, second, sub, subs, highs):
@@ -235,27 +239,27 @@
     return pl.BlockSpec(memory_space=pltpu.SMEM)
 
 
-def call_cells(got, diffused, slabs, subs):
+def call_cells(got, diffused, dest, slabs, subs):
     lines, lanes = diffused.shape[1:]
     f32 = functools.partial(jax.ShapeDtypeStruct, dtype=jnp.float32)
     return pl.pallas_call(
         functools.partial(cell_kernel, slabs=slabs, subs=subs),
-        out_shape=(f32((2 * subs, lines, lanes)), f32((slabs * CAP * subs, lanes))),
-        in_specs=[vmem(), vmem()],
-        out_specs=(vmem(), vmem()),
+        out_shape=(f32((subs, lines, lanes)), f32((slabs * CAP * subs, lanes)), jax.ShapeDtypeStruct(dest.shape, dest.dtype)),
+        in_specs=[vmem(), vmem(), vmem()],
+        out_specs=(vmem(), vmem(), vmem()),
         scratch_shapes=[
             pltpu.VMEM((4 * subs * lines // 2, 2 * lanes), jnp.float32),
             pltpu.VMEM((2 * subs * lines // 2, 2 * lanes), jnp.float32),
             pltpu.VMEM((2 * lanes, lanes), jnp.float32),
             pltpu.VMEM((slabs * CAP, lanes), jnp.float32),
             pltpu.VMEM((slabs * CAP, lanes), jnp.float32),
-            pltpu.VMEM((GROUP * 4 * subs, lanes), jnp.float32),
-            pltpu.VMEM((GROUP * 8, lanes), jnp.float32),
-            pltpu.SMEM((slabs * CAP + GROUP + CAP,), jnp.int32),
+            pltpu.VMEM((slabs * CAP * 4 * subs, lanes), jnp.float32),
+            pltpu.VMEM((slabs * CAP * 8, lanes), jnp.float32),
+            pltpu.SMEM((2 * slabs * CAP,), jnp.int32),
         ],
         compiler_params=small(8),
         name="cells",
-    )(got, diffused)
+    )(got, diffused, dest)
 
 
 def shards(field, diffusion, secrete, uptake, cell_voxel, block_dest):
@@ -285,19 +289,18 @@
     sent = sent.reshape(slabs, rows // 2, 2, cells)
     got = lax.all_to_all(sent, "gz", split_axis=0, concat_axis=0, tiled=True)
     diffused = diffuse(field, diffusion).reshape(subs, lines, lanes)
-    sums, back = call_cells(got.reshape(slabs * rows, cells), diffused, slabs, subs)
+    new, back, first = call_cells(got.reshape(slabs * rows, cells), diffused, block_dest.reshape(1, blocks) * CAP, slabs, subs)
     back = back.reshape(slabs, CAP * subs, cells)
     came = lax.all_to_all(back, "gz", split_axis=0, concat_axis=0, tiled=True)
-    cell_conc = pl.pallas_call(
+    cell_conc, new_field = pl.pallas_call(
         functools.partial(place_kernel, blocks=blocks, cells=cells, subs=subs),
-        out_shape=f32((subs, blocks * cells)),
-        in_specs=[smem(), vmem()],
-        out_specs=vmem(),
-        scratch_shapes=[pltpu.SMEM((slabs,), jnp.int32)],
+        out_shape=(f32((subs, blocks * cells)), f32(new.shape)),
+        in_specs=[smem(), vmem(), vmem()],
+        out_specs=(vmem(), vmem()),
+        scratch_shapes=[pltpu.SMEM((slabs * CAP,), jnp.int32)],
         compiler_params=small(4),
         name="place",
-    )(dest, came)
-    new_field = (diffused + sums[:subs]) / (1.0 + sums[subs:])
+    )(first.reshape(blocks), came.reshape(slabs * CAP * subs, cells), new)
     return (new_field.reshape(field.shape), cell_conc)
 
 

time: 102 us -> 100 us (0.980)
  the two profiles are of different devices: /device:TPU:80 before, /device:TPU:72 now
where the time goes in v5:
time: 100 us
  starting transfers between devices  54.7 us (55%)
  blocking collectives  24 us (24%)
  waiting for transfers between devices  15.1 us (15%)
  Pallas kernels  4.67 us (5%)
    all_to_all x1, starting transfers between devices, shards(): got = lax.all_to_all(sent, 'gz', split_axis=0, concat_axis=0, tiled=True)  43.8 us
    all_to_all x1, blocking collectives, shards(): came = lax.all_to_all(back, 'gz', split_axis=0, concat_axis=0, tiled=True)  24 us
    ppermute x2, starting transfers between devices, extended(): lax.ppermute(last, axis, up)  7.22 us
    ppermute x2, waiting for transfers between devices, extended(): lax.ppermute(leading, axis, [(b, a) for a, b in up])  6.06 us
    all_to_all x1, waiting for transfers between devices, shards(): got = lax.all_to_all(sent, 'gz', split_axis=0, concat_axis=0, tiled=True)  5.63 us
    ppermute x2, starting transfers between devices, extended(): lax.ppermute(leading, axis, [(b, a) for a, b in up])  3.65 us
    ppermute x2, waiting for transfers between devices, extended(): lax.ppermute(last, axis, up)  3.4 us
  transfers between devices with their start and end apart: 5, of which 4 were waited for; matrix products, arithmetic and copies ran while one was open for 0% of the time, Pallas kernels for 0%

profile of v5, /device:TPU:72, one launch (start us, length us, event | category | flops | bytes accessed | tf_op | source)
XLA Modules:
  0.0 100.0 jit_solution(16966318112259887303)
XLA Ops:
  0.6 1.8 %pack.1 = f32[864,128]{1,0:T(8,128)} custom-call(s32[32]{0:T(128)} %bitcast.18, f32[4,4096]{1,0:T(4,128)} %secrete_in.1, f32[4,4096]{1,0:T(4,128)} %uptake_in.1, s32[32,128]{1,0:T(8,128)} %bitcast.17), custom_call_target="tpu_custom_call" | custom-call | tf_op jit(solution)/shard_map/pack/pallas_call | solution.py:274
  2.5 0.0 copy-start
  2.5 43.8 %all-to-all-start = ((f32[16,27,2,128]{3,2,1,0:T(2,128)}), f32[16,27,2,128]{3,2,1,0:T(2,128)S(1)}, u32[]{:S(2)}, u32[]{:S(2)}) async-start(f32[16,27,2,128]{3,2,1,0:T(2,128)} %bitcast.16), calls=%async_computation | async-start | bytes 884736 | tf_op jit(solution)/shard_map/all_to_all | solution.py:290
  46.3 0.0 copy-done
  46.3 3.7 %collective-permute-start.1 = (f32[4,1,8,128]{3,2,1,0:T(8,128)S(1)}, f32[4,1,8,128]{3,2,1,0:T(8,128)S(1)}, u32[]{:S(2)}, u32[]{:S(2)}) collective-permute-start(f32[4,1,8,128]{3,2,1,0:T(8,128)S(1)} %get-tuple-element.15), channel_id=1, source_target_pairs={{0,16},{16,32},{32,48},{48,64},{64,80},{80,96},{96,112},{112,128},... | collective-permute-start | bytes 49160 | tf_op jit(solution)/shard_map/ppermute | solution.py:21
  50.0 1.3 %collective-permute-start = (f32[4,1,8,128]{3,2,1,0:T(8,128)S(1)}, f32[4,1,8,128]{3,2,1,0:T(8,128)S(1)}, u32[]{:S(2)}, u32[]{:S(2)}) collective-permute-start(f32[4,1,8,128]{3,2,1,0:T(8,128)S(1)} %get-tuple-element.14), channel_id=1, source_target_pairs={{16,0},{32,16},{48,32},{64,48},{80,64},{96,80},{112,96},{128,112},... | collective-permute-start | bytes 49160 | tf_op jit(solution)/shard_map/ppermute | solution.py:22
  51.3 0.0 copy-start.2
  51.3 2.3 %collective-permute-start.2 = (f32[4,4,1,128]{3,2,1,0:T(1,128)S(1)}, f32[4,4,1,128]{3,2,1,0:T(1,128)S(1)}, u32[]{:S(2)}, u32[]{:S(2)}) collective-permute-start(f32[4,4,1,128]{3,2,1,0:T(1,128)S(1)} %get-tuple-element.13), channel_id=1, source_target_pairs={{2,0},{4,2},{6,4},{8,6},{10,8},{12,10},{14,12},{3,1},{5,3},{7,5},{... | collective-permute-start | bytes 24584 | tf_op jit(solution)/shard_map/ppermute | solution.py:22
  53.7 3.6 %collective-permute-start.3 = (f32[4,4,1,128]{3,2,1,0:T(1,128)S(1)}, f32[4,4,1,128]{3,2,1,0:T(1,128)S(1)}, u32[]{:S(2)}, u32[]{:S(2)}) collective-permute-start(f32[4,4,1,128]{3,2,1,0:T(1,128)S(1)} %get-tuple-element.12), channel_id=1, source_target_pairs={{0,2},{2,4},{4,6},{6,8},{8,10},{10,12},{12,14},{1,3},{3,5},{5,7},{... | collective-permute-start | bytes 24584 | tf_op jit(solution)/shard_map/ppermute | solution.py:21
  57.3 0.0 copy-done.2
  57.3 0.0 collective-permute-done.2
  57.3 3.2 %collective-permute-done.3 = f32[4,4,1,128]{3,2,1,0:T(1,128)S(1)} collective-permute-done((f32[4,4,1,128]{3,2,1,0:T(1,128)S(1)}, f32[4,4,1,128]{3,2,1,0:T(1,128)S(1)}, u32[]{:S(2)}, u32[]{:S(2)}) %collective-permute-start.3) | collective-permute-done | bytes 8224 | tf_op jit(solution)/shard_map/ppermute | solution.py:21
  60.5 0.2 collective-permute-done.1
  60.7 6.1 %collective-permute-done = f32[4,1,8,128]{3,2,1,0:T(8,128)S(1)} collective-permute-done((f32[4,1,8,128]{3,2,1,0:T(8,128)S(1)}, f32[4,1,8,128]{3,2,1,0:T(8,128)S(1)}, u32[]{:S(2)}, u32[]{:S(2)}) %collective-permute-start) | collective-permute-done | bytes 16416 | tf_op jit(solution)/shard_map/ppermute | solution.py:22
  66.8 0.0 copy-start.1
  66.8 0.3 select_maximum_fusion
  67.1 0.4 copy-done.1
  67.4 0.1 fusion.4.diffused
  67.5 5.6 %all-to-all-done = f32[16,27,2,128]{3,2,1,0:T(2,128)S(1)} async-done(((f32[16,27,2,128]{3,2,1,0:T(2,128)}), f32[16,27,2,128]{3,2,1,0:T(2,128)S(1)}, u32[]{:S(2)}, u32[]{:S(2)}) %all-to-all-start) | async-done | bytes 442400 | tf_op jit(solution)/shard_map/all_to_all | solution.py:290
  73.2 1.5 %cells.1 = (f32[4,32,128]{2,1,0:T(8,128)S(1)}, f32[384,128]{1,0:T(8,128)S(1)}, s32[1,32]{1,0:T(1,128)S(1)}) custom-call(f32[864,128]{1,0:T(8,128)S(1)} %bitcast.12, f32[4,32,128]{2,1,0:T(8,128)S(1)} %fusion.4.diffused, s32[1,32]{1,0:T(1,128)S(1)} %multiply_bitcast_fusion.dest_in), custom_call_target="tpu_custom_call" | custom-call | tf_op jit(solution)/shard_map/cells/pallas_call | solution.py:245
  74.7 24.0 %all_to_all.10 = f32[16,24,128]{2,1,0:T(8,128)S(1)} all-to-all(f32[16,24,128]{2,1,0:T(8,128)S(1)} %bitcast.14), channel_id=1, replica_groups=mesh['grp'=2,'gz'=16,'gy'=8,'sa'=2] {'gz'}, dimensions={0} | all-to-all | bytes 393216 | tf_op jit(solution)/shard_map/all_to_all | solution.py:294
  98.7 1.3 %place.1 = (f32[4,4096]{1,0:T(4,128)}, f32[4,32,128]{2,1,0:T(8,128)}) custom-call(s32[32]{0:T(128)S(1)} %bitcast.15, f32[384,128]{1,0:T(8,128)S(1)} %bitcast.13, f32[4,32,128]{2,1,0:T(8,128)S(1)} %get-tuple-element.9.new), custom_call_target="tpu_custom_call" | custom-call | tf_op jit(solution)/shard_map/place/pallas_call | solution.py:295
  (8 shorter events, 0.1 us)
Async XLA Ops:
  2.5 43.8 %copy-start = (f32[4,4,8,128]{3,2,1,0:T(8,128)S(1)}, f32[4,4,8,128]{3,2,1,0:T(8,128)}, u32[]{:S(2)}) copy-start(f32[4,4,8,128]{3,2,1,0:T(8,128)} %param.6) | copy-start | bytes 196612
  2.5 70.7 %all-to-all-start = ((f32[16,27,2,128]{3,2,1,0:T(2,128)}), f32[16,27,2,128]{3,2,1,0:T(2,128)S(1)}, u32[]{:S(2)}, u32[]{:S(2)}) async-start(f32[16,27,2,128]{3,2,1,0:T(2,128)} %bitcast.16), calls=%async_computation | async-start | bytes 884736 | tf_op jit(solution)/shard_map/all_to_all | solution.py:290
  46.3 14.4 %collective-permute-start.1 = (f32[4,1,8,128]{3,2,1,0:T(8,128)S(1)}, f32[4,1,8,128]{3,2,1,0:T(8,128)S(1)}, u32[]{:S(2)}, u32[]{:S(2)}) collective-permute-start(f32[4,1,8,128]{3,2,1,0:T(8,128)S(1)} %get-tuple-element.15), channel_id=1, source_target_pairs={{0,16},{16,32},{32,48},{48,64},{64,80},{80,96},{96,112},{112,128},... | collective-permute-start | bytes 49160 | tf_op jit(solution)/shard_map/ppermute | solution.py:21
  50.0 16.8 %collective-permute-start = (f32[4,1,8,128]{3,2,1,0:T(8,128)S(1)}, f32[4,1,8,128]{3,2,1,0:T(8,128)S(1)}, u32[]{:S(2)}, u32[]{:S(2)}) collective-permute-start(f32[4,1,8,128]{3,2,1,0:T(8,128)S(1)} %get-tuple-element.14), channel_id=1, source_target_pairs={{16,0},{32,16},{48,32},{64,48},{80,64},{96,80},{112,96},{128,112},... | collective-permute-start | bytes 49160 | tf_op jit(solution)/shard_map/ppermute | solution.py:22
  51.3 5.9 %copy-start.2 = (s32[32,1]{0,1:T(1,128)S(1)}, s32[32,1]{0,1:T(1,128)}, u32[]{:S(2)}) copy-start(s32[32,1]{0,1:T(1,128)} %param.11) | copy-start | bytes 388
  51.3 5.9 %collective-permute-start.2 = (f32[4,4,1,128]{3,2,1,0:T(1,128)S(1)}, f32[4,4,1,128]{3,2,1,0:T(1,128)S(1)}, u32[]{:S(2)}, u32[]{:S(2)}) collective-permute-start(f32[4,4,1,128]{3,2,1,0:T(1,128)S(1)} %get-tuple-element.13), channel_id=1, source_target_pairs={{2,0},{4,2},{6,4},{8,6},{10,8},{12,10},{14,12},{3,1},{5,3},{7,5},{... | collective-permute-start | bytes 24584 | tf_op jit(solution)/shard_map/ppermute | solution.py:22
  53.7 6.8 %collective-permute-start.3 = (f32[4,4,1,128]{3,2,1,0:T(1,128)S(1)}, f32[4,4,1,128]{3,2,1,0:T(1,128)S(1)}, u32[]{:S(2)}, u32[]{:S(2)}) collective-permute-start(f32[4,4,1,128]{3,2,1,0:T(1,128)S(1)} %get-tuple-element.12), channel_id=1, source_target_pairs={{0,2},{2,4},{4,6},{6,8},{8,10},{10,12},{12,14},{1,3},{3,5},{5,7},{... | collective-permute-start | bytes 24584 | tf_op jit(solution)/shard_map/ppermute | solution.py:21
  66.8 0.7 copy-start.1

commit v6 on v5

--- a/solution.py
+++ b/solution.py
@@ -71,8 +71,9 @@
         out[pl.ds(to * rows + base + slot, 1), :] = voxel[b : b + 1, :].astype(jnp.float32)
 
 
-def place_kernel(first, came, new, out, new_field, used, *, blocks, cells, subs):
-    new_field[...] = new[...]
+def place_kernel(first, came, new, out, new_field, used, sem, *, blocks, cells, subs):
+    leave = pltpu.make_async_copy(new, new_field, sem)
+    leave.start()
     for i in range(0, came.shape[0] // subs, CAP):
         used[i] = i
     for b in range(blocks):
@@ -80,6 +81,7 @@
         slot = used[slab]
         used[slab] = slot + 1
         out[:, b * cells : (b + 1) * cells] = came[pl.ds(slot * subs, subs), :]
+    leave.wait()
 
 
 def halves(x):
@@ -87,7 +89,7 @@
     return high, (x - high.astype(jnp.float32)).astype(jnp.bfloat16)
 
 
-SIZES, PART = (32, 40, 48, 96), 2
+SIZES, PART = (18, 34, 48, 96), 2
 BITS = 10
 
 
@@ -296,8 +298,8 @@
         functools.partial(place_kernel, blocks=blocks, cells=cells, subs=subs),
         out_shape=(f32((subs, blocks * cells)), f32(new.shape)),
         in_specs=[smem(), vmem(), vmem()],
-        out_specs=(vmem(), vmem()),
-        scratch_shapes=[pltpu.SMEM((slabs * CAP,), jnp.int32)],
+        out_specs=(vmem(), pl.BlockSpec(memory_space=pltpu.HBM)),
+        scratch_shapes=[pltpu.SMEM((slabs * CAP,), jnp.int32), pltpu.SemaphoreType.DMA],
         compiler_params=small(4),
         name="place",
     )(first.reshape(blocks), came.reshape(slabs * CAP * subs, cells), new)

time: 100 us -> 99.9 us (level)
  the two profiles are of different devices: /device:TPU:72 before, /device:TPU:80 now
where the time goes in v6:
time: 99.9 us; the launch traced here: 100 us
  starting transfers between devices  54.7 us (55%)
  blocking collectives  23.6 us (24%)
  waiting for transfers between devices  15.1 us (15%)
  Pallas kernels  5.21 us (5%)
    all_to_all x1, starting transfers between devices, shards(): got = lax.all_to_all(sent, 'gz', split_axis=0, concat_axis=0, tiled=True)  43.8 us
    all_to_all x1, blocking collectives, shards(): came = lax.all_to_all(back, 'gz', split_axis=0, concat_axis=0, tiled=True)  23.6 us
    ppermute x2, starting transfers between devices, extended(): lax.ppermute(last, axis, up)  8.24 us
    ppermute x2, waiting for transfers between devices, extended(): lax.ppermute(leading, axis, [(b, a) for a, b in up])  6.06 us
    all_to_all x1, waiting for transfers between devices, shards(): got = lax.all_to_all(sent, 'gz', split_axis=0, concat_axis=0, tiled=True)  5.63 us
    ppermute x2, waiting for transfers between devices, extended(): lax.ppermute(last, axis, up)  3.4 us
    ppermute x2, starting transfers between devices, extended(): lax.ppermute(leading, axis, [(b, a) for a, b in up])  2.62 us
  transfers between devices with their start and end apart: 5, of which 4 were waited for; matrix products, arithmetic and copies ran while one was open for 0% of the time, Pallas kernels for 0%

profile of v6, /device:TPU:80, one launch (start us, length us, event | category | flops | bytes accessed | tf_op | source)
XLA Modules:
  0.0 100.2 jit_solution(17414714739124815738)
XLA Ops:
  0.6 1.8 %pack.1 = f32[864,128]{1,0:T(8,128)} custom-call(s32[32]{0:T(128)} %bitcast.18, f32[4,4096]{1,0:T(4,128)} %secrete_in.1, f32[4,4096]{1,0:T(4,128)} %uptake_in.1, s32[32,128]{1,0:T(8,128)} %bitcast.17), custom_call_target="tpu_custom_call" | custom-call | tf_op jit(solution)/shard_map/pack/pallas_call | solution.py:276
  2.5 0.0 copy-start
  2.5 43.8 %all-to-all-start = ((f32[16,27,2,128]{3,2,1,0:T(2,128)}), f32[16,27,2,128]{3,2,1,0:T(2,128)S(1)}, u32[]{:S(2)}, u32[]{:S(2)}) async-start(f32[16,27,2,128]{3,2,1,0:T(2,128)} %bitcast.16), calls=%async_computation | async-start | bytes 884736 | tf_op jit(solution)/shard_map/all_to_all | solution.py:292
  46.3 0.0 copy-done
  46.3 3.7 %collective-permute-start.1 = (f32[4,1,8,128]{3,2,1,0:T(8,128)S(1)}, f32[4,1,8,128]{3,2,1,0:T(8,128)S(1)}, u32[]{:S(2)}, u32[]{:S(2)}) collective-permute-start(f32[4,1,8,128]{3,2,1,0:T(8,128)S(1)} %get-tuple-element.15), channel_id=1, source_target_pairs={{0,16},{16,32},{32,48},{48,64},{64,80},{80,96},{96,112},{112,128},... | collective-permute-start | bytes 49160 | tf_op jit(solution)/shard_map/ppermute | solution.py:21
  50.0 1.3 %collective-permute-start = (f32[4,1,8,128]{3,2,1,0:T(8,128)S(1)}, f32[4,1,8,128]{3,2,1,0:T(8,128)S(1)}, u32[]{:S(2)}, u32[]{:S(2)}) collective-permute-start(f32[4,1,8,128]{3,2,1,0:T(8,128)S(1)} %get-tuple-element.14), channel_id=1, source_target_pairs={{16,0},{32,16},{48,32},{64,48},{80,64},{96,80},{112,96},{128,112},... | collective-permute-start | bytes 49160 | tf_op jit(solution)/shard_map/ppermute | solution.py:22
  51.3 0.0 copy-start.2
  51.3 1.3 %collective-permute-start.2 = (f32[4,4,1,128]{3,2,1,0:T(1,128)S(1)}, f32[4,4,1,128]{3,2,1,0:T(1,128)S(1)}, u32[]{:S(2)}, u32[]{:S(2)}) collective-permute-start(f32[4,4,1,128]{3,2,1,0:T(1,128)S(1)} %get-tuple-element.13), channel_id=1, source_target_pairs={{2,0},{4,2},{6,4},{8,6},{10,8},{12,10},{14,12},{3,1},{5,3},{7,5},{... | collective-permute-start | bytes 24584 | tf_op jit(solution)/shard_map/ppermute | solution.py:22
  52.7 4.6 %collective-permute-start.3 = (f32[4,4,1,128]{3,2,1,0:T(1,128)S(1)}, f32[4,4,1,128]{3,2,1,0:T(1,128)S(1)}, u32[]{:S(2)}, u32[]{:S(2)}) collective-permute-start(f32[4,4,1,128]{3,2,1,0:T(1,128)S(1)} %get-tuple-element.12), channel_id=1, source_target_pairs={{0,2},{2,4},{4,6},{6,8},{8,10},{10,12},{12,14},{1,3},{3,5},{5,7},{... | collective-permute-start | bytes 24584 | tf_op jit(solution)/shard_map/ppermute | solution.py:21
  57.3 0.0 copy-done.2
  57.3 0.0 collective-permute-done.2
  57.3 1.3 %collective-permute-done.3 = f32[4,4,1,128]{3,2,1,0:T(1,128)S(1)} collective-permute-done((f32[4,4,1,128]{3,2,1,0:T(1,128)S(1)}, f32[4,4,1,128]{3,2,1,0:T(1,128)S(1)}, u32[]{:S(2)}, u32[]{:S(2)}) %collective-permute-start.3) | collective-permute-done | bytes 8224 | tf_op jit(solution)/shard_map/ppermute | solution.py:21
  58.6 2.1 %collective-permute-done.1 = f32[4,1,8,128]{3,2,1,0:T(8,128)S(1)} collective-permute-done((f32[4,1,8,128]{3,2,1,0:T(8,128)S(1)}, f32[4,1,8,128]{3,2,1,0:T(8,128)S(1)}, u32[]{:S(2)}, u32[]{:S(2)}) %collective-permute-start.1) | collective-permute-done | bytes 16416 | tf_op jit(solution)/shard_map/ppermute | solution.py:21
  60.7 6.1 %collective-permute-done = f32[4,1,8,128]{3,2,1,0:T(8,128)S(1)} collective-permute-done((f32[4,1,8,128]{3,2,1,0:T(8,128)S(1)}, f32[4,1,8,128]{3,2,1,0:T(8,128)S(1)}, u32[]{:S(2)}, u32[]{:S(2)}) %collective-permute-start) | collective-permute-done | bytes 16416 | tf_op jit(solution)/shard_map/ppermute | solution.py:22
  66.8 0.0 copy-start.1
  66.8 0.3 select_maximum_fusion
  67.1 0.4 copy-done.1
  67.4 0.1 fusion.4.diffused
  67.5 5.6 %all-to-all-done = f32[16,27,2,128]{3,2,1,0:T(2,128)S(1)} async-done(((f32[16,27,2,128]{3,2,1,0:T(2,128)}), f32[16,27,2,128]{3,2,1,0:T(2,128)S(1)}, u32[]{:S(2)}, u32[]{:S(2)}) %all-to-all-start) | async-done | bytes 442400 | tf_op jit(solution)/shard_map/all_to_all | solution.py:292
  73.2 1.6 %cells.1 = (f32[4,32,128]{2,1,0:T(8,128)S(1)}, f32[384,128]{1,0:T(8,128)S(1)}, s32[1,32]{1,0:T(1,128)S(1)}) custom-call(f32[864,128]{1,0:T(8,128)S(1)} %bitcast.12, f32[4,32,128]{2,1,0:T(8,128)S(1)} %fusion.4.diffused, s32[1,32]{1,0:T(1,128)S(1)} %multiply_bitcast_fusion.dest_in), custom_call_target="tpu_custom_call" | custom-call | tf_op jit(solution)/shard_map/cells/pallas_call | solution.py:247
  74.8 23.6 %all_to_all.10 = f32[16,24,128]{2,1,0:T(8,128)S(1)} all-to-all(f32[16,24,128]{2,1,0:T(8,128)S(1)} %bitcast.14), channel_id=1, replica_groups=mesh['grp'=2,'gz'=16,'gy'=8,'sa'=2] {'gz'}, dimensions={0} | all-to-all | bytes 393216 | tf_op jit(solution)/shard_map/all_to_all | solution.py:296
  98.4 1.8 %place.1 = (f32[4,4096]{1,0:T(4,128)}, f32[4,32,128]{2,1,0:T(8,128)}) custom-call(s32[32]{0:T(128)S(1)} %bitcast.15, f32[384,128]{1,0:T(8,128)S(1)} %bitcast.13, f32[4,32,128]{2,1,0:T(8,128)S(1)} %get-tuple-element.9.new), custom_call_target="tpu_custom_call" | custom-call | tf_op jit(solution)/shard_map/place/pallas_call | solution.py:297
  (8 shorter events, 0.1 us)
Async XLA Ops:
  2.5 43.8 %copy-start = (f32[4,4,8,128]{3,2,1,0:T(8,128)S(1)}, f32[4,4,8,128]{3,2,1,0:T(8,128)}, u32[]{:S(2)}) copy-start(f32[4,4,8,128]{3,2,1,0:T(8,128)} %param.6) | copy-start | bytes 196612
  2.5 70.7 %all-to-all-start = ((f32[16,27,2,128]{3,2,1,0:T(2,128)}), f32[16,27,2,128]{3,2,1,0:T(2,128)S(1)}, u32[]{:S(2)}, u32[]{:S(2)}) async-start(f32[16,27,2,128]{3,2,1,0:T(2,128)} %bitcast.16), calls=%async_computation | async-start | bytes 884736 | tf_op jit(solution)/shard_map/all_to_all | solution.py:292
  46.3 14.4 %collective-permute-start.1 = (f32[4,1,8,128]{3,2,1,0:T(8,128)S(1)}, f32[4,1,8,128]{3,2,1,0:T(8,128)S(1)}, u32[]{:S(2)}, u32[]{:S(2)}) collective-permute-start(f32[4,1,8,128]{3,2,1,0:T(8,128)S(1)} %get-tuple-element.15), channel_id=1, source_target_pairs={{0,16},{16,32},{32,48},{48,64},{64,80},{80,96},{96,112},{112,128},... | collective-permute-start | bytes 49160 | tf_op jit(solution)/shard_map/ppermute | solution.py:21
  50.0 16.8 %collective-permute-start = (f32[4,1,8,128]{3,2,1,0:T(8,128)S(1)}, f32[4,1,8,128]{3,2,1,0:T(8,128)S(1)}, u32[]{:S(2)}, u32[]{:S(2)}) collective-permute-start(f32[4,1,8,128]{3,2,1,0:T(8,128)S(1)} %get-tuple-element.14), channel_id=1, source_target_pairs={{16,0},{32,16},{48,32},{64,48},{80,64},{96,80},{112,96},{128,112},... | collective-permute-start | bytes 49160 | tf_op jit(solution)/shard_map/ppermute | solution.py:22
  51.3 5.9 %copy-start.2 = (s32[32,1]{0,1:T(1,128)S(1)}, s32[32,1]{0,1:T(1,128)}, u32[]{:S(2)}) copy-start(s32[32,1]{0,1:T(1,128)} %param.11) | copy-start | bytes 388
  51.3 5.9 %collective-permute-start.2 = (f32[4,4,1,128]{3,2,1,0:T(1,128)S(1)}, f32[4,4,1,128]{3,2,1,0:T(1,128)S(1)}, u32[]{:S(2)}, u32[]{:S(2)}) collective-permute-start(f32[4,4,1,128]{3,2,1,0:T(1,128)S(1)} %get-tuple-element.13), channel_id=1, source_target_pairs={{2,0},{4,2},{6,4},{8,6},{10,8},{12,10},{14,12},{3,1},{5,3},{7,5},{... | collective-permute-start | bytes 24584 | tf_op jit(solution)/shard_map/ppermute | solution.py:22
  52.7 5.9 %collective-permute-start.3 = (f32[4,4,1,128]{3,2,1,0:T(1,128)S(1)}, f32[4,4,1,128]{3,2,1,0:T(1,128)S(1)}, u32[]{:S(2)}, u32[]{:S(2)}) collective-permute-start(f32[4,4,1,128]{3,2,1,0:T(1,128)S(1)} %get-tuple-element.12), channel_id=1, source_target_pairs={{0,2},{2,4},{4,6},{6,8},{8,10},{10,12},{12,14},{1,3},{3,5},{5,7},{... | collective-permute-start | bytes 24584 | tf_op jit(solution)/shard_map/ppermute | solution.py:21
  66.8 0.7 copy-start.1
